TPU v7x, 16 devices: a whole 2x2x2 slice. The times are simulated.
16 devices in a mesh: sp: 16 (over z, y, x, core).
Axes of the slice: x: 2, y: 2, z: 2, core: 2. Of those that a mesh axis runs over, the one named last changes fastest.
Arguments:
- x: bfloat16 [3, 4096, 2048], P(None, 'sp')
- ln1_w: bfloat16 [2048], replicated
- w_qkv: bfloat16 [2048, 6144], replicated
- q_ln_w: bfloat16 [16, 128], replicated
- k_ln_w: bfloat16 [16, 128], replicated
- w_out: bfloat16 [2048, 2048], replicated
- grad_y: bfloat16 [3, 4096, 2048], P(None, 'sp')
Outputs:
- output 1: bfloat16 [3, 4096, 2048], P(None, 'sp')
- output 2: bfloat16 [3, 4096, 2048], P(None, 'sp')
- output 3: float32 [2048], replicated
- output 4: float32 [2048, 6144], replicated
- output 5: float32 [16, 128], replicated
- output 6: float32 [16, 128], replicated
- output 7: float32 [2048, 2048], replicated
All inputs are finite; a program needn't handle non-finite values.
Results may differ from a plain program's by a relative error of at most 0.0129169.
Values are sent between devices in bfloat16 or wider.
A program may use at most 1 GiB of HBM per device.

v0:
```python
import math
import jax
import jax.numpy as jnp
from jax import lax
from jax.sharding import PartitionSpec as P


def alibi_slopes(n_heads):
    pow_two = 2 ** math.ceil(math.log2(n_heads))
    exponents = jnp.arange(1, pow_two + 1, dtype=jnp.float32) * (8.0 / pow_two)
    slopes = jnp.exp2(-exponents)
    if pow_two != n_heads:
        slopes = jnp.concatenate([slopes[1::2], slopes[0::2]])[:n_heads]
    return slopes


def layer_norm(values, weight):
    centered = values - jnp.mean(values, axis=-1, keepdims=True)
    var_val = jnp.mean(centered * centered, axis=-1, keepdims=True)
    return centered * lax.rsqrt(var_val + 1e-5) * weight


def block_scores(q_cur, k_all, slopes, q_start, score_scale):
    q_count = q_cur.shape[1]
    k_count = k_all.shape[1]
    scores = jnp.einsum('bqhd,bkhd->bhqk', q_cur, k_all, preferred_element_type=jnp.float32) * score_scale
    pos_gap = (q_start + jnp.arange(q_count))[:, None] - jnp.arange(k_count)[None, :]
    biased = scores - slopes[:, None, None] * pos_gap.astype(jnp.float32)
    return jnp.where(pos_gap >= 0, biased, -1e30)


def attn_forward(q_loc, k_all, v_all, slopes, q_offset, q_blk):
    n_batch, q_len, n_heads, head_dim = q_loc.shape
    n_blk = q_len // q_blk
    score_scale = head_dim ** -0.5
    q_blocks = q_loc.reshape(n_batch, n_blk, q_blk, n_heads, head_dim)

    def one_block(blk_idx):
        q_cur = lax.dynamic_index_in_dim(q_blocks, blk_idx, axis=1, keepdims=False)
        scores = block_scores(q_cur, k_all, slopes, q_offset + blk_idx * q_blk, score_scale)
        row_max = jnp.max(scores, axis=-1)
        weights = jnp.exp(scores - row_max[..., None])
        row_sum = jnp.sum(weights, axis=-1)
        weighted = jnp.einsum('bhqk,bkhd->bqhd', weights.astype(jnp.bfloat16), v_all, preferred_element_type=jnp.float32)
        out_blk = weighted / jnp.swapaxes(row_sum, 1, 2)[..., None]
        return out_blk.astype(jnp.bfloat16), row_max + jnp.log(row_sum)

    out_blocks, lse_blocks = lax.map(one_block, jnp.arange(n_blk))
    out_all = jnp.moveaxis(out_blocks, 0, 1).reshape(n_batch, q_len, n_heads, head_dim)
    return out_all, lse_blocks


def attn_backward(q_loc, k_all, v_all, out_all, d_out, lse_blocks, slopes, q_offset, q_blk):
    n_batch, q_len, n_heads, head_dim = q_loc.shape
    n_blk = q_len // q_blk
    score_scale = head_dim ** -0.5
    q_blocks = q_loc.reshape(n_batch, n_blk, q_blk, n_heads, head_dim)
    do_blocks = d_out.reshape(n_batch, n_blk, q_blk, n_heads, head_dim)
    row_dot = jnp.einsum('bqhd,bqhd->bhq', d_out, out_all, preferred_element_type=jnp.float32).reshape(n_batch, n_heads, n_blk, q_blk)

    def one_block(acc_pair, blk_idx):
        dk_acc, dv_acc = acc_pair
        q_cur = lax.dynamic_index_in_dim(q_blocks, blk_idx, axis=1, keepdims=False)
        do_cur = lax.dynamic_index_in_dim(do_blocks, blk_idx, axis=1, keepdims=False)
        delta_cur = lax.dynamic_index_in_dim(row_dot, blk_idx, axis=2, keepdims=False)
        lse_cur = lax.dynamic_index_in_dim(lse_blocks, blk_idx, axis=0, keepdims=False)
        scores = block_scores(q_cur, k_all, slopes, q_offset + blk_idx * q_blk, score_scale)
        prob_blk = jnp.exp(scores - lse_cur[..., None])
        dv_acc = dv_acc + jnp.einsum('bhqk,bqhd->bkhd', prob_blk.astype(jnp.bfloat16), do_cur, preferred_element_type=jnp.float32)
        d_probs = jnp.einsum('bqhd,bkhd->bhqk', do_cur, v_all, preferred_element_type=jnp.float32)
        d_scores = (prob_blk * (d_probs - delta_cur[..., None]) * score_scale).astype(jnp.bfloat16)
        dq_cur = jnp.einsum('bhqk,bkhd->bqhd', d_scores, k_all, preferred_element_type=jnp.float32)
        dk_acc = dk_acc + jnp.einsum('bhqk,bqhd->bkhd', d_scores, q_cur, preferred_element_type=jnp.float32)
        return (dk_acc, dv_acc), dq_cur.astype(jnp.bfloat16)

    zero_acc = jnp.zeros(k_all.shape, jnp.float32)
    acc_final, dq_blocks = lax.scan(one_block, (zero_acc, zero_acc), jnp.arange(n_blk))
    d_q = jnp.moveaxis(dq_blocks, 0, 1).reshape(n_batch, q_len, n_heads, head_dim)
    return d_q, acc_final[0], acc_final[1]


def solution(mesh):
    n_sp = mesh.shape['sp']
    seq_spec = P(None, 'sp', None)
    rep_spec = P()

    def local_step(x, ln1_w, w_qkv, q_ln_w, k_ln_w, w_out, grad_y):
        n_batch, tok_loc, d_model = x.shape
        n_heads, head_dim = q_ln_w.shape
        heads_loc = n_heads // n_sp
        seq_len = tok_loc * n_sp
        head_base = lax.axis_index('sp') * heads_loc
        slopes = lax.dynamic_slice_in_dim(alibi_slopes(n_heads), head_base, heads_loc)
        head_shape = (n_batch, tok_loc, n_heads, head_dim)
        flat_shape = (n_batch, tok_loc, d_model)
        x_f32 = x.astype(jnp.float32)
        h_f32, ln1_pull = jax.vjp(layer_norm, x_f32, ln1_w.astype(jnp.float32))
        h_act = h_f32.astype(jnp.bfloat16)
        qkv_raw = jnp.einsum('btd,de->bte', h_act, w_qkv, preferred_element_type=jnp.float32)
        q_f32, q_pull = jax.vjp(layer_norm, qkv_raw[..., :d_model], q_ln_w.reshape(d_model).astype(jnp.float32))
        k_f32, k_pull = jax.vjp(layer_norm, qkv_raw[..., d_model:2 * d_model], k_ln_w.reshape(d_model).astype(jnp.float32))
        qkv_tok = jnp.stack([q_f32.astype(jnp.bfloat16).reshape(head_shape), k_f32.astype(jnp.bfloat16).reshape(head_shape), qkv_raw[..., 2 * d_model:].astype(jnp.bfloat16).reshape(head_shape)])
        qkv_head = lax.all_to_all(qkv_tok, 'sp', 3, 2, tiled=True)
        q_blk = math.gcd(seq_len, 256)
        o_head, lse_blocks = attn_forward(qkv_head[0], qkv_head[1], qkv_head[2], slopes, 0, q_blk)
        o_tok = lax.all_to_all(o_head, 'sp', 1, 2, tiled=True).reshape(flat_shape)
        y = (jnp.einsum('btd,de->bte', o_tok, w_out, preferred_element_type=jnp.float32) + x_f32).astype(jnp.bfloat16)
        grad_w_out = jnp.einsum('btd,bte->de', o_tok, grad_y, preferred_element_type=jnp.float32)
        d_o = jnp.einsum('bte,de->btd', grad_y, w_out, preferred_element_type=jnp.float32).astype(jnp.bfloat16)
        d_o_head = lax.all_to_all(d_o.reshape(head_shape), 'sp', 2, 1, tiled=True)
        d_q, d_k, d_v = attn_backward(qkv_head[0], qkv_head[1], qkv_head[2], o_head, d_o_head, lse_blocks, slopes, 0, q_blk)
        d_qkv_head = jnp.stack([d_q, d_k.astype(jnp.bfloat16), d_v.astype(jnp.bfloat16)])
        d_qkv_tok = lax.all_to_all(d_qkv_head, 'sp', 2, 3, tiled=True)
        dq_raw, grad_q_ln = q_pull(d_qkv_tok[0].reshape(flat_shape).astype(jnp.float32))
        dk_raw, grad_k_ln = k_pull(d_qkv_tok[1].reshape(flat_shape).astype(jnp.float32))
        d_qkv = jnp.concatenate([dq_raw.astype(jnp.bfloat16), dk_raw.astype(jnp.bfloat16), d_qkv_tok[2].reshape(flat_shape)], axis=-1)
        grad_w_qkv = jnp.einsum('btd,bte->de', h_act, d_qkv, preferred_element_type=jnp.float32)
        d_h = jnp.einsum('bte,de->btd', d_qkv, w_qkv, preferred_element_type=jnp.float32).astype(jnp.bfloat16)
        d_x_norm, grad_ln1 = ln1_pull(d_h.astype(jnp.float32))
        grad_x = (d_x_norm + grad_y.astype(jnp.float32)).astype(jnp.bfloat16)
        weight_grads = lax.psum((grad_ln1, grad_w_qkv, grad_q_ln.reshape(n_heads, head_dim), grad_k_ln.reshape(n_heads, head_dim), grad_w_out), 'sp')
        return (y, grad_x) + tuple(weight_grads)

    return jax.shard_map(local_step, mesh=mesh, in_specs=(seq_spec, rep_spec, rep_spec, rep_spec, rep_spec, rep_spec, seq_spec), out_specs=(seq_spec, seq_spec, rep_spec, rep_spec, rep_spec, rep_spec, rep_spec), check_vma=False)
```

profile of v0, /device:TPU:0, one launch (start us, length us, event | category | flops | bytes accessed | tf_op | source)
XLA Modules:
  0.0 2318.8 jit_solution(2523902825052095578)
XLA Ops:
  7.2 10.1 fusion.110
  28.6 23.2 fusion.81
  83.5 114.9 %all-to-all-done = bf16[3,3,256,16,128]{4,2,1,0,3:T(8,128)(2,1)} async-done(((bf16[3,3,256,16,128]{4,2,1,0,3:T(8,128)(2,1)}), bf16[3,3,256,16,128]{4,2,1,0,3:T(8,128)(2,1)}, u32[]{:S(2)}, u32[]{:S(2)}) %all-to-all-start) | async-done | bytes 9437216 | tf_op jit(solution)/shard_map/all_to_all | solution.py:103
  198.4 11.1 copy.109
  219.9 386.3 %while.27 = (s32[]{:T(128)}, bf16[16,3,256,1,128]{4,2,0,1,3:T(8,128)(2,1)}, f32[16,3,1,256]{3,1,2,0:T(4,128)S(1)}, s32[16]{0:T(128)S(1)}, bf16[3,16,256,1,128]{4...) while((s32[]{:T(128)}, ...), condition=%wide.region_9.10_spmd, body=%wide.region_6.9_spmd.sunk | while | flops 1660091904 | bytes 94796024 | solution.py:48
  624.3 712.4 %while.28 = (s32[]{:T(128)}, f32[3,4096,1,128]{1,3,0,2:T(8,128)}, f32[3,4096,1,128]{1,3,0,2:T(8,128)}, bf16[16,3,256,1,128]{4,2,0,1,3:T(8,128)(2,1)}, s32[16]{0:...) while((s32[]{:T(128)}, f32[3,4096,1,128]{1,3,0,2:T(8,128)}, ...), condition=%wide.region_11.12_spmd.clone, body=%wide.region_10.11_spmd.clone.sunk | while | flops 4079059200 | bytes 133128472 | solution.py:77
  637.1 11.5 multiply_convert_fusion.4
  678.7 11.5 multiply_convert_fusion.4
  690.2 10.8 bitcast_add_fusion.5
  723.4 11.5 multiply_convert_fusion.4
  734.9 10.8 bitcast_add_fusion.5
  768.1 11.5 multiply_convert_fusion.4
  779.6 10.8 bitcast_add_fusion.5
  812.8 11.5 multiply_convert_fusion.4
  824.3 10.8 bitcast_add_fusion.5
  857.6 11.5 multiply_convert_fusion.4
  869.1 10.8 bitcast_add_fusion.5
  902.3 11.5 multiply_convert_fusion.4
  913.8 10.8 bitcast_add_fusion.5
  947.0 11.5 multiply_convert_fusion.4
  958.5 10.8 bitcast_add_fusion.5
  991.7 11.5 multiply_convert_fusion.4
  1003.2 10.8 bitcast_add_fusion.5
  1036.5 11.5 multiply_convert_fusion.4
  1048.0 10.8 bitcast_add_fusion.5
  1081.2 11.5 multiply_convert_fusion.4
  1092.7 10.8 bitcast_add_fusion.5
  1125.9 11.5 multiply_convert_fusion.4
  1137.4 10.8 bitcast_add_fusion.5
  1170.6 11.5 multiply_convert_fusion.4
  1182.1 10.8 bitcast_add_fusion.5
  1215.3 11.5 multiply_convert_fusion.4
  1226.9 10.8 bitcast_add_fusion.5
  1260.1 11.5 multiply_convert_fusion.4
  1271.6 10.8 bitcast_add_fusion.5
  1304.8 11.5 multiply_convert_fusion.4
  1316.3 10.8 bitcast_add_fusion.5
  1352.1 63.0 %copy.81 = bf16[3,3,4096,1,128]{4,1,3,0,2:T(4,128)(2,1)} copy(bf16[3,3,4096,1,128]{4,2,1,3,0:T(8,128)(2,1)S(1)} %pad_maximum_fusion.1) | data formatting | bytes 18874368 | tf_op jit(solution)/shard_map/stack | solution.py:112
  1427.4 12.7 convolution_bitcast_fusion.1
  1440.2 134.9 %all-to-all-done.3 = bf16[3,3,4096,1,128]{4,1,3,0,2:T(4,128)(2,1)} async-done(((bf16[3,3,4096,1,128]{4,1,3,0,2:T(4,128)(2,1)}), bf16[3,3,4096,1,128]{4,1,3,0,2:T(4,128)(2,1)}, u32[]{:S(2)}, u32[]{:S(2)}) %all-to-all-start.3) | async-done | bytes 9437216 | tf_op jit(solution)/shard_map/all_to_all | solution.py:113
  1575.1 15.8 copy.108
  1644.5 31.0 %convolution_bitcast_fusion = f32[2048,6144]{1,0:T(8,128)} fusion(bf16[3,256,2048]{2,1,0:T(8,128)(2,1)} %reshape_squeeze.10, bf16[3,256,2048]{2,1,0:T(8,128)(2,1)} %get-tuple-element.269, bf16[3,256,2048]{2,1,0:T(8,128)(2,1)} %get-tuple-element.268, bf16[3,256,2048]{2,1,0:T(8,128)(2,1)} %param.11, f32[2048]{0:T(1024)S(1)} %copy-done.17, ...), kind=kOutput, calls=%fused_computation.64 | convolution fusion | flops 19363528704 | bytes 62928896 | tf_op jit(solution)/shard_map/btd,bte->de/dot_general | solution.py:117
  1677.4 11.9 fusion.97
  1689.2 27.4 %fusion.96 = (f32[3,256]{1,0:T(4,128)S(1)}, bf16[3,256,2048]{2,1,0:T(8,128)(2,1)}) fusion(bf16[3,256,2048]{2,1,0:T(8,128)(2,1)S(1)} %copy-done.5, f32[2048]{0:T(1024)S(1)} %copy-done.17, f32[3,256]{1,0:T(4,128)S(1)} %copy-done.19, bf16[2048,6144]{1,0:T(8,128)(2,1)} %param.13, bf16[3,256,2048]{2,1,0:T(8,128)(2,1)} %reshape_squeeze.10, ...), kind=kOutput, calls=%fused_computation.96 | convolution fusion | flops 19366674432 | bytes 40908800 | tf_op jit(solution)/shard_map/bte,de->btd/dot_general | solution.py:118
  1721.4 34.5 %all-reduce = (f32[2048]{0:T(1024)}, f32[16,128]{1,0:T(8,128)}, f32[16,128]{1,0:T(8,128)}) all-reduce(f32[2048]{0:T(1024)S(1)} %get-tuple-element.219, f32[16,128]{1,0:T(8,128)S(1)} %bitcast.278, f32[16,128]{1,0:T(8,128)S(1)} %bitcast.277), channel_id=1, replica_groups=mesh['sp'=16] {'sp'}, use_global_device_ids=true, to_apply=%region_19.20 | all-reduce | flops 6144 | bytes 49152 | tf_op jit(solution)/shard_map/psum | solution.py:121
  1761.7 503.8 %all-reduce.4.cloned.1.call-done = (f32[2048,6144]{1,0:T(8,128)}, f32[2048,2048]{1,0:T(8,128)}) async-done(((f32[2048,6144]{1,0:T(8,128)}, f32[2048,2048]{1,0:T(8,128)}), (f32[2048,6144]{1,0:T(8,128)}, f32[2048,2048]{1,0:T(8,128)})) %all-reduce.4.cloned.1.call-update) | async-done | bytes 67108880 | tf_op jit(solution)/shard_map/psum | solution.py:121
  2265.4 34.5 %copy.138 = f32[2048,6144]{1,0:T(8,128)} copy(f32[2048,6144]{1,0:T(8,128)} %get-tuple-element.499) | data formatting | bytes 100663296
  2299.9 11.8 copy.139
  (509 shorter events, 832.4 us)
Async XLA Ops:
  17.3 8.1 copy-start.4
  19.8 7.6 copy-start.32
  19.8 55.1 %all-to-all-start.2 = ((bf16[3,256,16,128]{3,1,0,2:T(8,128)(2,1)}), bf16[3,256,16,128]{3,1,0,2:T(8,128)(2,1)}, u32[]{:S(2)}, u32[]{:S(2)}) async-start(bf16[3,256,16,128]{3,1,0,2:T(8,128)(2,1)} %bitcast.267), calls=%async_computation.2 | async-start | bytes 6291456 | tf_op jit(solution)/shard_map/all_to_all | solution.py:110
  51.8 6.9 copy-start.2
  74.9 123.5 %all-to-all-start = ((bf16[3,3,256,16,128]{4,2,1,0,3:T(8,128)(2,1)}), bf16[3,3,256,16,128]{4,2,1,0,3:T(8,128)(2,1)}, u32[]{:S(2)}, u32[]{:S(2)}) async-start(bf16[3,3,256,16,128]{4,2,1,0,3:T(8,128)(2,1)} %pad_maximum_fusion), calls=%async_computation | async-start | bytes 18874368 | tf_op jit(solution)/shard_map/all_to_all | solution.py:103
  232.2 6.4 copy-start
  256.4 6.4 copy-start
  280.5 6.4 copy-start
  304.6 6.4 copy-start
  328.8 6.4 copy-start
  352.9 6.4 copy-start
  377.1 6.4 copy-start
  401.2 6.4 copy-start
  425.4 6.4 copy-start
  449.5 6.4 copy-start
  612.9 802.1 %all-to-all-start.1 = ((bf16[3,4096,1,128]{3,0,2,1:T(4,128)(2,1)}), bf16[3,4096,1,128]{3,0,2,1:T(4,128)(2,1)}, u32[]{:S(2)}, u32[]{:S(2)}) async-start(bf16[3,4096,1,128]{3,0,2,1:T(4,128)(2,1)} %copy.71), calls=%async_computation.1 | async-start | bytes 8388608 | tf_op jit(solution)/shard_map/all_to_all | solution.py:106
  648.6 9.7 copy-start.1
  690.2 10.8 copy-start.1
  734.9 10.8 copy-start.1
  779.6 10.8 copy-start.1
  824.3 10.8 copy-start.1
  869.1 10.8 copy-start.1
  913.8 10.8 copy-start.1
  958.5 10.8 copy-start.1
  1003.2 10.8 copy-start.1
  1048.0 10.8 copy-start.1
  1092.7 10.8 copy-start.1
  1137.4 10.8 copy-start.1
  1182.1 10.8 copy-start.1
  1226.8 10.8 copy-start.1
  1271.6 10.8 copy-start.1
  1316.3 10.8 copy-start.1
  1415.0 160.1 %all-to-all-start.3 = ((bf16[3,3,4096,1,128]{4,1,3,0,2:T(4,128)(2,1)}), bf16[3,3,4096,1,128]{4,1,3,0,2:T(4,128)(2,1)}, u32[]{:S(2)}, u32[]{:S(2)}) async-start(bf16[3,3,4096,1,128]{4,1,3,0,2:T(4,128)(2,1)} %copy.81), calls=%async_computation.3 | async-start | bytes 25165824 | tf_op jit(solution)/shard_map/all_to_all | solution.py:113
  1419.0 846.4 %all-reduce.4.cloned.1.call-start = ((), (), s32[]{:S(2)}) async-start(), calls=%async_computation.4 | async-start | bytes 134217728 | tf_op jit(solution)/shard_map/psum | solution.py:121
  1609.2 7.1 copy-start.9
  1609.2 7.1 copy-start.13
  1609.2 12.9 copy-start.31
  1616.4 15.4 slice-start
  1616.4 15.4 slice-start.1
  1622.8 9.0 copy-start.29
  1622.8 9.1 slice-start.2
  1622.8 9.9 slice-start.3
  1622.8 11.1 slice-start.4
  1622.8 11.1 copy-start.21
  1636.3 8.1 copy-start.17
  1636.3 8.1 copy-start.19
  1636.3 8.1 copy-start.25
  1689.2 27.4 %copy-start.27 = (f32[3,256]{1,0:T(4,128)S(1)}, f32[3,256]{1,0:T(4,128)}, u32[]{:S(2)}) copy-start(f32[3,256]{1,0:T(4,128)} %copy-done.26) | copy-start | bytes 9220
  (42 other events, 205.9 us)
Sparse Core Ops, SparseCore 0:
  1675.6 589.7 all-reduce.3
where the time goes:
time: 2330 us; the launch traced here: 2320 us
  matrix products  911 us (39%)
  waiting for transfers between devices  754 us (32%)
  other arithmetic  266 us (11%)
  local copies, waits for them, and re-layouts  237 us (10%)
  loops' own time  84.4 us (4%)
  blocking collectives  34.5 us (1%)
    psum x1, waiting for transfers between devices, local_step(): lax.psum((grad_ln1, grad_w_qkv, grad_q_ln.reshape(n_heads, head_dim), gra...  504 us
    dot_general x32, matrix products, block_scores(): jnp.einsum('bqhd,bkhd->bhqk', q_cur, k_all, preferred_element_type=jnp.fl...  201 us
    dot_general x16, matrix products, one_block(): jnp.einsum('bqhd,bkhd->bhqk', do_cur, v_all, preferred_element_type=jnp.f...  184 us
    dot_general x16, matrix products, one_block(): jnp.einsum('bhqk,bqhd->bkhd', prob_blk.astype(jnp.bfloat16), do_cur, pref...  172 us
    all_to_all x1, waiting for transfers between devices, local_step(): d_qkv_tok = lax.all_to_all(d_qkv_head, 'sp', 2, 3, tiled=True)  135 us
    all_to_all x1, waiting for transfers between devices, local_step(): qkv_head = lax.all_to_all(qkv_tok, 'sp', 3, 2, tiled=True)  115 us
    dot_general x16, matrix products, one_block(): jnp.einsum('bhqk,bqhd->bkhd', d_scores, q_cur, preferred_element_type=jnp...  111 us
    reduce_sum x16, other arithmetic, one_block(): row_sum = jnp.sum(weights, axis=-1)  102 us
  transfers between devices with their start and end apart: 5, of which 3 were waited for; matrix products, arithmetic and copies ran while one was open for 38% of the time, Pallas kernels for 0%

commit v1 on v0

v1 whole, which is shorter than its diff:
```python
import functools, math
import jax
import jax.numpy as jnp
from jax import lax
from jax.experimental import pallas as pl
from jax.experimental.pallas import tpu as pltpu
from jax.sharding import PartitionSpec as P

def attn_kernel(blk, tok, slope_ref, q_ref, k_ref, v_ref, do_ref, out_ref, kt_ref, vt_ref, s_ref, dp_ref, dk_ref, dv_ref, acc_ref):
    i = pl.program_id(0)
    n_blk = pl.num_programs(0)
    head_dim = q_ref.shape[1]
    f32, bf16 = jnp.float32, jnp.bfloat16
    scale = head_dim ** -0.5
    log2e = math.log2(math.e)
    slope2 = slope_ref[0] * log2e
    nt = (((1,), (1,)), ((), ()))

    def rows(j):
        return pl.ds(pl.multiple_of(j * blk, blk), blk)

    @pl.when(i == 0)
    def _():
        def fill(j, c):
            sl = rows(j)
            kt_ref[:, sl] = k_ref[sl, :].T
            vt_ref[:, sl] = v_ref[sl, :].T
            dk_ref[sl, :] = jnp.zeros((blk, head_dim), f32)
            dv_ref[sl, :] = jnp.zeros((blk, head_dim), f32)
            return c
        lax.fori_loop(0, n_blk, fill, 0)

    q = q_ref[...]
    do = do_ref[...]

    def lanes(col):
        return jnp.concatenate([col] * (blk // col.shape[1]), axis=1)

    def pass_a(j, mx, diag):
        sl = rows(j)
        s = lax.dot_general(k_ref[sl, :], q, nt, preferred_element_type=f32)
        row = lax.broadcasted_iota(jnp.int32, (blk, 128), 0)
        gap = (row + (j - i) * blk).astype(f32) * slope2
        s = s * (scale * log2e) + lanes(gap)
        if diag:
            key = lax.broadcasted_iota(jnp.int32, (blk, blk), 0)
            qry = lax.broadcasted_iota(jnp.int32, (blk, blk), 1)
            s = jnp.where(key <= qry, s, -1e30)
        s_ref[sl, :] = s
        dp_ref[sl, :] = lax.dot_general(v_ref[sl, :], do, nt, preferred_element_type=f32)
        return jnp.maximum(mx, jnp.max(s.reshape(blk // 8, 8, blk), axis=0))

    mx = lax.fori_loop(0, i, lambda j, c: pass_a(j, c, False), jnp.full((8, blk), -1e30, f32))
    mx = pass_a(i, mx, True)
    mx = jnp.max(mx, axis=0, keepdims=True)

    acc_ref[...] = jnp.zeros(acc_ref.shape, f32)

    def pass_b(j, c):
        tot, dlt = c
        sl = rows(j)
        p = jnp.exp2(s_ref[sl, :] - mx)
        s_ref[sl, :] = p
        acc_ref[...] += jnp.dot(vt_ref[:, sl], p.astype(bf16), preferred_element_type=f32)
        tot = tot + jnp.sum(p.reshape(blk // 8, 8, blk), axis=0)
        dlt = dlt + jnp.sum((p * dp_ref[sl, :]).reshape(blk // 8, 8, blk), axis=0)
        return tot, dlt

    zero = jnp.zeros((8, blk), f32)
    tot, dlt = lax.fori_loop(0, i + 1, pass_b, (zero, zero))
    inv = 1.0 / jnp.sum(tot, axis=0, keepdims=True)
    dlt = jnp.sum(dlt, axis=0, keepdims=True) * inv
    n_tok = blk // tok
    o_blk = (acc_ref[...] * inv).T.astype(bf16)
    for t in range(n_tok):
        out_ref[i * n_tok + t, 0] = o_blk[t * tok:(t + 1) * tok]

    acc_ref[...] = jnp.zeros(acc_ref.shape, f32)

    def pass_c(j, c):
        sl = rows(j)
        p = s_ref[sl, :] * inv
        dv_ref[sl, :] += jnp.dot(p.astype(bf16), do, preferred_element_type=f32)
        ds = (p * (dp_ref[sl, :] - dlt)).astype(bf16)
        dk_ref[sl, :] += jnp.dot(ds, q, preferred_element_type=f32)
        acc_ref[...] += jnp.dot(kt_ref[:, sl], ds, preferred_element_type=f32)
        return c

    lax.fori_loop(0, i + 1, pass_c, 0)
    dq_blk = (acc_ref[...] * scale).T.astype(bf16)
    for t in range(n_tok):
        out_ref[i * n_tok + t, 1] = dq_blk[t * tok:(t + 1) * tok]

    @pl.when(i == n_blk - 1)
    def _():
        for t in range(n_blk * n_tok):
            out_ref[t, 2] = (dk_ref[t * tok:(t + 1) * tok, :] * scale).astype(bf16)
            out_ref[t, 3] = dv_ref[t * tok:(t + 1) * tok, :].astype(bf16)


def attention(q, k, v, do, slope, tok, blk=512):
    seq, head_dim = q.shape
    n_blk = seq // blk
    full = pl.BlockSpec((seq, head_dim), lambda i: (0, 0))
    part = pl.BlockSpec((blk, head_dim), lambda i: (i, 0))
    pairs = seq * (seq + blk) // 2
    f32, bf16 = jnp.float32, jnp.bfloat16
    return pl.pallas_call(
        functools.partial(attn_kernel, blk, tok),
        grid=(n_blk,),
        out_shape=jax.ShapeDtypeStruct((seq // tok, 4, tok, head_dim), bf16),
        in_specs=[pl.BlockSpec(memory_space=pltpu.SMEM), part, full, full, part],
        out_specs=pl.BlockSpec((seq // tok, 4, tok, head_dim), lambda i: (0, 0, 0, 0)),
        scratch_shapes=[
            pltpu.VMEM((head_dim, seq), bf16), pltpu.VMEM((head_dim, seq), bf16),
            pltpu.VMEM((seq, blk), f32), pltpu.VMEM((seq, blk), f32),
            pltpu.VMEM((seq, head_dim), f32), pltpu.VMEM((seq, head_dim), f32),
            pltpu.VMEM((head_dim, blk), f32),
        ],
        compiler_params=pltpu.CompilerParams(dimension_semantics=("arbitrary",), vmem_limit_bytes=56 * 2 ** 20),
        cost_estimate=pl.CostEstimate(flops=12 * pairs * head_dim * 2, bytes_accessed=8 * seq * head_dim * 2, transcendentals=pairs),
        name="attn_fwd_bwd",
    )(slope, q, k, v, do)


def alibi_slopes(n_heads):
    pow_two = 2 ** math.ceil(math.log2(n_heads))
    exponents = jnp.arange(1, pow_two + 1, dtype=jnp.float32) * (8.0 / pow_two)
    slopes = jnp.exp2(-exponents)
    if pow_two != n_heads:
        slopes = jnp.concatenate([slopes[1::2], slopes[0::2]])[:n_heads]
    return slopes


def layer_norm(values, weight):
    centered = values - jnp.mean(values, axis=-1, keepdims=True)
    var_val = jnp.mean(centered * centered, axis=-1, keepdims=True)
    return centered * lax.rsqrt(var_val + 1e-5) * weight


def head_stats(raw):
    mean = jnp.mean(raw, axis=(0, 2))
    centered = raw - mean[None, :, None]
    return mean, lax.rsqrt(jnp.mean(centered * centered, axis=(0, 2)) + 1e-5)


def solution(mesh):
    n_sp = mesh.shape['sp']
    seq_spec = P(None, 'sp', None)
    rep_spec = P()

    def local_step(x, ln1_w, w_qkv, q_ln_w, k_ln_w, w_out, grad_y):
        f32, bf16 = jnp.float32, jnp.bfloat16
        n_batch, tok, d_model = x.shape
        n_heads, head_dim = q_ln_w.shape
        assert n_heads == n_sp
        seq = tok * n_sp
        me = lax.axis_index('sp')
        slope = lax.dynamic_slice_in_dim(alibi_slopes(n_heads), me, 1)
        w_out3 = w_out.reshape(n_heads, head_dim, d_model)
        w_qkv4 = w_qkv.reshape(d_model, 3, n_heads, head_dim)
        w_head = lax.dynamic_slice_in_dim(w_qkv4, me, 1, axis=2).reshape(d_model, 3 * head_dim)
        ln_w3 = (q_ln_w.astype(f32)[:, None, :], k_ln_w.astype(f32)[:, None, :])
        ln_head = tuple(lax.dynamic_slice_in_dim(w.astype(f32), me, 1, axis=0) for w in (q_ln_w, k_ln_w))
        x_f32 = x.astype(f32)
        ln1_f32 = ln1_w.astype(f32)

        h_act, h_all = [], []
        for b in range(n_batch):
            h_act.append(layer_norm(x_f32[b], ln1_f32).astype(bf16))
            h_all.append(lax.all_gather(h_act[b], 'sp', axis=0, tiled=True))

        do_head = []
        for b in range(n_batch):
            d_o = jnp.einsum('te,hde->htd', grad_y[b], w_out3, preferred_element_type=f32).astype(bf16)
            do_head.append(lax.all_to_all(d_o, 'sp', 0, 0, tiled=True).reshape(seq, head_dim))

        raw_tok, stats_tok = [], []
        for b in range(n_batch):
            raw = [jnp.einsum('te,ehd->htd', h_act[b], w_qkv4[:, n], preferred_element_type=f32) for n in range(2)]
            raw_tok.append(raw)
            stats_tok.append([head_stats(r) for r in raw])
        stats = jnp.stack([jnp.stack([s for pair in st for s in pair]) for st in stats_tok])
        stats_all = lax.all_gather(stats, 'sp')
        stats_all = jnp.moveaxis(stats_all, 0, 2).reshape(n_batch, 4, seq)

        outs, back, xhat = [], [], []
        for b in range(n_batch):
            raw = jnp.dot(h_all[b], w_head, preferred_element_type=f32)
            hat = [(raw[:, n * head_dim:(n + 1) * head_dim] - stats_all[b, 2 * n][:, None]) * stats_all[b, 2 * n + 1][:, None] for n in range(2)]
            xhat.append(hat)
            q, k = [(hat[n] * ln_head[n]).astype(bf16) for n in range(2)]
            v = raw[:, 2 * head_dim:].astype(bf16)
            out = attention(q, k, v, do_head[b], slope, tok)
            outs.append(out)
            back.append(lax.all_to_all(out, 'sp', 0, 0, tiled=True))

        o_tok = jnp.stack([t[:, 0] for t in back])
        grad_w_out = lax.psum(jnp.einsum('bhtd,bte->hde', o_tok, grad_y, preferred_element_type=f32).reshape(d_model, d_model), 'sp')

        y, grad_x, means, ln_grads = [], [], [], []
        for b in range(n_batch):
            t = back[b]
            y.append((jnp.einsum('htd,hde->te', t[:, 0], w_out3, preferred_element_type=f32) + x_f32[b]).astype(bf16))
            parts, mean_b, ln_b = [], [], []
            for n in range(2):
                mean, rstd = stats_tok[b][n]
                hat = (raw_tok[b][n] - mean[None, :, None]) * rstd[None, :, None]
                g = t[:, 1 + n].astype(f32)
                gw = g * ln_w3[n]
                c1 = jnp.mean(gw, axis=(0, 2))
                c2 = jnp.mean(gw * hat, axis=(0, 2))
                mean_b += [c1, c2]
                ln_b.append(jnp.sum(g * hat, axis=1))
                parts.append(((gw - c1[None, :, None] - hat * c2[None, :, None]) * rstd[None, :, None]).astype(bf16))
            parts.append(t[:, 3])
            means.append(jnp.stack(mean_b))
            d_qkv = jnp.concatenate(parts, axis=0)
            d_h = jnp.einsum('ctd,ecd->te', d_qkv, w_qkv.reshape(d_model, 3 * n_heads, head_dim), preferred_element_type=f32).astype(bf16)
            _, ln1_pull = jax.vjp(layer_norm, x_f32[b], ln1_f32)
            d_x, g_ln1 = ln1_pull(d_h.astype(f32))
            ln_grads.append((g_ln1, ln_b[0], ln_b[1]))
            grad_x.append((d_x + grad_y[b].astype(f32)).astype(bf16))

        means_all = jnp.moveaxis(lax.all_gather(jnp.stack(means), 'sp'), 0, 2).reshape(n_batch, 4, seq)

        def w_grad(cols):
            total = sum(lax.dot_general(h_all[b], cols[b], (((0,), (0,)), ((), ())), preferred_element_type=f32) for b in range(n_batch))
            return lax.all_gather(total, 'sp')

        pieces = [w_grad([outs[b][:, 3].reshape(seq, head_dim) for b in range(n_batch)])]
        for n in (1, 0):
            cols = []
            for b in range(n_batch):
                gw = outs[b][:, 1 + n].reshape(seq, head_dim).astype(f32) * ln_head[n]
                rstd = stats_all[b, 2 * n + 1][:, None]
                cols.append(((gw - means_all[b, 2 * n][:, None] - xhat[b][n] * means_all[b, 2 * n + 1][:, None]) * rstd).astype(bf16))
            pieces.append(w_grad(cols))
        grad_w_qkv = jnp.concatenate([jnp.moveaxis(p, 0, 1).reshape(d_model, d_model) for p in pieces[::-1]], axis=1)

        small = lax.psum(tuple(sum(g[m] for g in ln_grads) for m in range(3)), 'sp')
        return (jnp.stack(y), jnp.stack(grad_x), small[0], grad_w_qkv, small[1], small[2], grad_w_out)

    return jax.shard_map(local_step, mesh=mesh, in_specs=(seq_spec, rep_spec, rep_spec, rep_spec, rep_spec, rep_spec, seq_spec), out_specs=(seq_spec, seq_spec, rep_spec, rep_spec, rep_spec, rep_spec, rep_spec), check_vma=False)
```

time: 2330 us -> 1100 us (0.47)
  matrix products: 911 us -> 261 us
  waiting for transfers between devices: 754 us -> 195 us
  other arithmetic: 266 us -> 87.8 us
  blocking collectives: 34.5 us -> 208 us
  Pallas kernels: 0 us -> 167 us
  local copies, waits for them, and re-layouts: 237 us -> 146 us
  loops' own time: 84.4 us -> 0 us
    dot_general x118 -> x22, matrix products: 911 us -> 214 us  [the longest x9 90.3 us: w_grad(): lax.dot_general(h_all[b], cols[b], (((0,), (0,)), ((), ())), preferred_el...]
    psum x1, waiting for transfers between devices: 504 us -> 107 us  [local_step(): lax.psum(jnp.einsum('bhtd,bte->hde', o_tok, grad_y, preferred_element_typ...]
    pallas_call x0 -> x3, Pallas kernels: none -> 167 us  [attention(): pl.pallas_call(functools.partial(attn_kernel, blk, tok), grid=(n_blk,), o...]
    all_to_all x4, waiting for transfers between devices: 250 us -> 86 us  [the longest x1 50 us: local_step(): back.append(lax.all_to_all(out, 'sp', 0, 0, tiled=True))]
    all_to_all x0 -> x2, blocking collectives: none -> 147 us  [local_step(): back.append(lax.all_to_all(out, 'sp', 0, 0, tiled=True))]
    reduce_sum x20 -> x8, other arithmetic: 124 us -> 11.9 us  [the longest x2 9.84 us: local_step(): ln_b.append(jnp.sum(g * hat, axis=1))]
    another operation x2 -> x0, loops' own time: 84.4 us -> none  [the longest x1 42.3 us: attn_forward(): out_blocks, lse_blocks = lax.map(one_block, jnp.arange(n_blk))]
    mul x32 -> x0, other arithmetic: 74.1 us -> none  [block_scores(): biased = scores - slopes[:, None, None] * pos_gap.astype(jnp.float32)]
  transfers between devices with their start and end apart: 5 -> 11, of which waited for: 3 -> 4; matrix products, arithmetic and copies ran while one was open for 38% -> 38% of each run, Pallas kernels for 0% -> 5%
where the time goes in v1:
time: 1100 us
  matrix products  261 us (24%)
  blocking collectives  208 us (19%)
  waiting for transfers between devices  195 us (18%)
  Pallas kernels  167 us (15%)
  local copies, waits for them, and re-layouts  146 us (13%)
  other arithmetic  87.8 us (8%)
  between operations  16.3 us (1%)
  starting transfers between devices  14.5 us (1%)
    pallas_call x3, Pallas kernels, attention(): pl.pallas_call(functools.partial(attn_kernel, blk, tok), grid=(n_blk,), o...  167 us
    all_to_all x2, blocking collectives, local_step(): back.append(lax.all_to_all(out, 'sp', 0, 0, tiled=True))  147 us
    psum x1, waiting for transfers between devices, local_step(): lax.psum(jnp.einsum('bhtd,bte->hde', o_tok, grad_y, preferred_element_typ...  107 us
    dot_general x9, matrix products, w_grad(): lax.dot_general(h_all[b], cols[b], (((0,), (0,)), ((), ())), preferred_el...  90.3 us
    unnamed x252, local copies, waits for them, and re-layouts  55.4 us
    all_to_all x1, waiting for transfers between devices, local_step(): back.append(lax.all_to_all(out, 'sp', 0, 0, tiled=True))  50 us
    unnamed x6, matrix products  46.9 us
    dot_general x3, matrix products, local_step(): jnp.einsum('ctd,ecd->te', d_qkv, w_qkv.reshape(d_model, 3 * n_heads, head...  41.1 us
  transfers between devices with their start and end apart: 11, of which 4 were waited for; matrix products, arithmetic and copies ran while one was open for 38% of the time, Pallas kernels for 5%

profile of v1, /device:TPU:0, one launch (start us, length us, event | category | flops | bytes accessed | tf_op | source)
XLA Modules:
  0.0 1095.0 jit_solution(17614850257671155311)
XLA Ops:
  17.0 7.1 fusion.162
  24.0 5.8 all-to-all-start.4
  29.8 32.6 %copy.82 = bf16[2048,6144]{0,1:T(8,128)(2,1)} copy(bf16[2048,6144]{1,0:T(8,128)(2,1)} %param.9) | data formatting | bytes 50331648 | tf_op args[2]
  62.4 9.6 fusion.243
  71.9 7.1 bitcast_reduce_fusion
  80.9 8.6 bitcast_reduce_fusion.4
  92.4 7.8 bitcast_reduce_fusion.2
  103.1 7.8 bitcast_reduce_fusion.1
  113.9 7.8 bitcast_reduce_fusion.5
  124.7 7.8 bitcast_reduce_fusion.3
  141.5 14.0 %all-gather = f32[48,4,256]{2,1,0:T(4,128)S(1)} all-gather(f32[3,4,256]{2,1,0:T(4,128)S(1)} %pad_maximum_fusion.3), channel_id=2, replica_groups=mesh['sp'=16] {'sp'}, dimensions={0}, use_global_device_ids=true | all-gather | bytes 208896 | tf_op jit(solution)/shard_map/all_gather | solution.py:184
  156.1 7.0 fusion.161
  168.5 7.0 fusion.160
  175.5 17.8 %all-to-all-done.2 = bf16[16,256,128]{1,2,0:T(8,128)(2,1)S(1)} async-done(((bf16[16,256,128]{1,2,0:T(8,128)(2,1)}), bf16[16,256,128]{1,2,0:T(8,128)(2,1)S(1)}, u32[]{:S(2)}, u32[]{:S(2)}) %all-to-all-start.2) | async-done | bytes 1048608 | tf_op jit(solution)/shard_map/all_to_all | solution.py:176
  199.0 18.2 %all-to-all-done = bf16[16,256,128]{1,2,0:T(8,128)(2,1)S(1)} async-done(((bf16[16,256,128]{1,2,0:T(8,128)(2,1)}), bf16[16,256,128]{1,2,0:T(8,128)(2,1)S(1)}, u32[]{:S(2)}, u32[]{:S(2)}) %all-to-all-start) | async-done | bytes 1048608 | tf_op jit(solution)/shard_map/all_to_all | solution.py:176
  218.5 12.6 %fusion.251 = f32[4096,384]{1,0:T(8,128)S(1)} fusion(bf16[4096,2048]{1,0:T(8,128)(2,1)} %all-gather.16.cloned.1.call-done, bf16[2048,384]{0,1:T(8,128)(2,1)} %bitcast.510), kind=kOutput, calls=%fused_computation.380 | convolution fusion | flops 6442450944 | bytes 24641536 | tf_op jit(solution)/shard_map/dot_general | solution.py:189
  235.6 12.1 %fusion.250 = f32[4096,384]{1,0:T(8,128)S(1)} fusion(bf16[4096,2048]{1,0:T(8,128)(2,1)} %all-gather.14.cloned.1.call-done, bf16[2048,384]{0,1:T(8,128)(2,1)S(1)} %bitcast.511), kind=kOutput, calls=%fused_computation.379 | convolution fusion | flops 6442450944 | bytes 24641536 | tf_op jit(solution)/shard_map/dot_general | solution.py:189
  253.9 55.7 %attn_fwd_bwd.4 = bf16[16,4,256,128]{3,2,1,0:T(8,128)(2,1)} custom-call(f32[1]{0:T(128)} %dynamic_slice.12.slope_ref, bf16[4096,128]{1,0:T(8,128)(2,1)} %get-tuple-element.71.q_ref, bf16[4096,128]{1,0:T(8,128)(2,1)} %get-tuple-element.70.k_ref, bf16[4096,128]{1,0:T(8,128)(2,1)} %slice.525.v_ref, bf16[4096,128]{1,0:T(8,128)(2,1)} %bitcast.515), custom_call_target="tpu_custom_call" | custom-call | flops 28991029248 | bytes 8388608 | tf_op jit(solution)/shard_map/attn_fwd_bwd/pallas_call | solution.py:108
  313.2 12.3 %fusion.249 = f32[4096,384]{1,0:T(8,128)S(1)} fusion(bf16[4096,2048]{1,0:T(8,128)(2,1)} %all-gather.12.cloned.1.call-done, bf16[2048,384]{0,1:T(8,128)(2,1)S(1)} %bitcast.512), kind=kOutput, calls=%fused_computation.378 | convolution fusion | flops 6442450944 | bytes 24641536 | tf_op jit(solution)/shard_map/dot_general | solution.py:189
  326.7 8.0 multiply_convert_fusion
  334.6 55.7 %attn_fwd_bwd.3 = bf16[16,4,256,128]{3,2,1,0:T(8,128)(2,1)} custom-call(f32[1]{0:T(128)} %dynamic_slice.12.slope_ref, bf16[4096,128]{1,0:T(8,128)(2,1)} %get-tuple-element.128.q_ref, bf16[4096,128]{1,0:T(8,128)(2,1)} %get-tuple-element.129.k_ref, bf16[4096,128]{1,0:T(8,128)(2,1)} %slice.526.v_ref, bf16[4096,128]{1,0:T(8,128)(2,1)} %bitcast.514), custom_call_target="tpu_custom_call" | custom-call | flops 28991029248 | bytes 8388608 | tf_op jit(solution)/shard_map/attn_fwd_bwd/pallas_call | solution.py:108
  393.9 55.8 %attn_fwd_bwd.5 = bf16[16,4,256,128]{3,2,1,0:T(8,128)(2,1)} custom-call(f32[1]{0:T(128)} %dynamic_slice.12.slope_ref, bf16[4096,128]{1,0:T(8,128)(2,1)} %get-tuple-element.73.q_ref, bf16[4096,128]{1,0:T(8,128)(2,1)} %get-tuple-element.72.k_ref, bf16[4096,128]{1,0:T(8,128)(2,1)} %slice.524.v_ref, bf16[4096,128]{1,0:T(8,128)(2,1)} %bitcast.513), custom_call_target="tpu_custom_call" | custom-call | flops 28991029248 | bytes 8388608 | tf_op jit(solution)/shard_map/attn_fwd_bwd/pallas_call | solution.py:108
  453.3 8.3 fusion.252
  461.6 8.8 convolution_add_fusion.1
  470.5 5.8 convolution_add_fusion
  476.3 66.8 %all_to_all.30 = bf16[16,4,256,128]{3,2,1,0:T(8,128)(2,1)} all-to-all(bf16[16,4,256,128]{3,2,1,0:T(8,128)(2,1)} %attn_fwd_bwd.4), channel_id=1, replica_groups=mesh['sp'=16] {'sp'}, dimensions={0} | all-to-all | bytes 8388608 | tf_op jit(solution)/shard_map/all_to_all | solution.py:196
  543.1 79.8 %all_to_all.31 = bf16[16,4,256,128]{3,2,1,0:T(8,128)(2,1)} all-to-all(bf16[16,4,256,128]{3,2,1,0:T(8,128)(2,1)S(1)} %copy-done.9), channel_id=1, replica_groups=mesh['sp'=16] {'sp'}, dimensions={0} | all-to-all | bytes 8388608 | tf_op jit(solution)/shard_map/all_to_all | solution.py:196
  630.1 50.0 %all-to-all-done.1 = bf16[16,4,256,128]{3,2,1,0:T(8,128)(2,1)} async-done(((bf16[16,4,256,128]{3,2,1,0:T(8,128)(2,1)}), bf16[16,4,256,128]{3,2,1,0:T(8,128)(2,1)}, u32[]{:S(2)}, u32[]{:S(2)}) %all-to-all-start.1) | async-done | bytes 4194336 | tf_op jit(solution)/shard_map/all_to_all | solution.py:196
  680.2 6.4 fusion.119
  687.3 15.0 %all-gather.1 = f32[48,4,256]{2,1,0:T(4,128)S(1)} all-gather(f32[3,4,256]{2,1,0:T(4,128)S(1)} %pad_maximum_fusion.4), channel_id=3, replica_groups=mesh['sp'=16] {'sp'}, dimensions={0}, use_global_device_ids=true | all-gather | bytes 208896 | tf_op jit(solution)/shard_map/all_gather | solution.py:225
  702.5 11.8 %fusion.169 = f32[2048,128]{1,0:T(8,128)S(1)} fusion(bf16[4096,2048]{1,0:T(8,128)(2,1)} %all-gather.12.cloned.1.call-done, bf16[4096,128]{1,0:T(8,128)(2,1)S(1)} %bitcast.521, f32[4096,384]{1,0:T(8,128)} %copy-done.12, f32[4096]{0:T(1024)S(1)} %bitcast.575, f32[4096]{0:T(1024)S(1)} %bitcast.576, f32[128]{0:T(128)S(1)} %copy-done.106, ...), kind=kOutput, calls=%fused_computation.241 | convolution fusion | flops 2152202240 | bytes 21037568 | tf_op jit(solution)/shard_map/dot_general | solution.py:228
  714.4 11.7 %convolution_add_fusion.5 = f32[2048,128]{1,0:T(8,128)S(1)} fusion(f32[2048,128]{1,0:T(8,128)S(1)} %fusion.169, bf16[4096,2048]{1,0:T(8,128)(2,1)} %all-gather.14.cloned.1.call-done, bf16[4096,128]{1,0:T(8,128)(2,1)S(1)} %bitcast.519, f32[4096,384]{1,0:T(8,128)} %copy-done.13, f32[4096]{0:T(1024)S(1)} %bitcast.573, f32[4096]{0:T(1024)S(1)} %bitcast.574, ...), kind=kOutput, calls=%fused_computation.105 | convolution fusion | flops 2152464384 | bytes 22086144 | tf_op jit(solution)/shard_map/dot_general | solution.py:228
  726.2 9.6 convolution_add_fusion.4
  735.9 12.1 %fusion.173 = f32[2048,128]{1,0:T(8,128)S(1)} fusion(bf16[4096,2048]{1,0:T(8,128)(2,1)} %all-gather.12.cloned.1.call-done, bf16[4096,128]{1,0:T(8,128)(2,1)} %bitcast.518, f32[4096,384]{1,0:T(8,128)} %copy-done.12, f32[4096]{0:T(1024)S(1)} %bitcast.569, f32[4096]{0:T(1024)S(1)} %bitcast.570, f32[128]{0:T(128)S(1)} %copy-done.104, f32[4096]{0:T(1024)S(1)} %bitcast.540, ...), kind=kOutput, calls=%fused_computation.242 | convolution fusion | flops 2152202240 | bytes 21037568 | tf_op jit(solution)/shard_map/dot_general | solution.py:228
  748.1 11.8 %convolution_add_fusion.3 = f32[2048,128]{1,0:T(8,128)S(1)} fusion(f32[2048,128]{1,0:T(8,128)S(1)} %fusion.173, bf16[4096,2048]{1,0:T(8,128)(2,1)} %all-gather.14.cloned.1.call-done, bf16[4096,128]{1,0:T(8,128)(2,1)S(1)} %bitcast.516, f32[4096,384]{1,0:T(8,128)} %copy-done.13, f32[4096]{0:T(1024)S(1)} %bitcast.567, f32[4096]{0:T(1024)S(1)} %bitcast.568, ...), kind=kOutput, calls=%fused_computation.103 | convolution fusion | flops 2152464384 | bytes 22086144 | tf_op jit(solution)/shard_map/dot_general | solution.py:228
  760.0 10.3 convolution_add_fusion.2
  777.4 10.7 fusion.24
  793.5 12.5 %fusion.75 = bf16[256,2048]{1,0:T(8,128)(2,1)S(1)} fusion(bf16[16,256,128]{2,1,0:T(8,128)(2,1)} %get-tuple-element.77, bf16[16,256,128]{2,1,0:T(8,128)(2,1)} %get-tuple-element.92, bf16[16,256,128]{2,1,0:T(8,128)(2,1)} %get-tuple-element.91, bf16[2048,6144]{1,0:T(8,128)(2,1)} %param.9), kind=kOutput, calls=%fused_computation.89 | convolution fusion | flops 6446120960 | bytes 29360128 | tf_op jit(solution)/shard_map/ctd,ecd->te/dot_general | solution.py:219
  810.9 13.3 %fusion.80 = bf16[256,2048]{1,0:T(8,128)(2,1)} fusion(bf16[16,256,128]{2,1,0:T(8,128)(2,1)} %get-tuple-element.75, bf16[16,256,128]{2,1,0:T(8,128)(2,1)} %get-tuple-element.90, bf16[16,256,128]{2,1,0:T(8,128)(2,1)} %get-tuple-element.89, bf16[2048,6144]{1,0:T(8,128)(2,1)} %param.9), kind=kOutput, calls=%fused_computation.90 | convolution fusion | flops 6446120960 | bytes 29360128 | tf_op jit(solution)/shard_map/ctd,ecd->te/dot_general | solution.py:219
  828.9 15.2 %fusion.99 = (f32[2048]{0:T(1024)S(1)}, f32[256]{0:T(256)S(1)}, f32[256]{0:T(256)S(1)}, f32[2048]{0:T(1024)S(1)}, f32[256]{0:T(256)S(1)}, /*index=5*/f32[2048]{0:T(1024)S(1)}, bf16[256,2048]{1,0:T(8,128)(2,1)S(1)}) fusion(f32[3,256,2048]{2,1,0:T(8,128)} %copy-done, f32[256]{0:T(256)S(1)} %copy-done.72, f32[256]{0:T(256)S(1)} %copy-done.64, ...), kind=kOutput, calls=%fused_computation.111 | convolution fusion | flops 6458697728 | bytes 37790720 | tf_op jit(solution)/shard_map/ctd,ecd->te/dot_general | solution.py:219
  844.2 32.0 %all-reduce = (f32[2048]{0:T(1024)}, f32[16,128]{1,0:T(8,128)}, f32[16,128]{1,0:T(8,128)}) all-reduce(f32[2048]{0:T(1024)S(1)} %add_add_fusion.5, f32[16,128]{1,0:T(8,128)S(1)} %add_add_fusion.4, f32[16,128]{1,0:T(8,128)S(1)} %add_add_fusion.3), channel_id=1, replica_groups=mesh['sp'=16] {'sp'}, use_global_device_ids=true, to_apply=%region_39.0 | all-reduce | flops 6144 | bytes 49152 | tf_op jit(solution)/shard_map/psum | solution.py:241
  880.4 6.8 fusion.92
  900.3 11.9 %copy.158 = f32[16,256,8,128]{3,2,0,1:T(8,128)} copy(f32[16,256,8,128]{3,2,1,0:T(8,128)} %bitcast.494) | data formatting | bytes 33554432 | tf_op jit(solution)/shard_map/reshape | solution.py:239
  912.2 11.8 %copy.160 = f32[16,256,8,128]{3,2,0,1:T(8,128)} copy(f32[16,256,8,128]{3,2,1,0:T(8,128)} %bitcast.495) | data formatting | bytes 33554432 | tf_op jit(solution)/shard_map/reshape | solution.py:239
  924.0 11.9 %copy.159 = f32[16,256,8,128]{3,2,0,1:T(8,128)} copy(f32[16,256,8,128]{3,2,1,0:T(8,128)} %bitcast.496) | data formatting | bytes 33554432 | tf_op jit(solution)/shard_map/reshape | solution.py:239
  935.9 33.1 %pad_maximum_fusion = f32[2048,6144]{1,0:T(8,128)} fusion(f32[2048,2048]{1,0:T(8,128)} %bitcast.491, f32[2048,2048]{1,0:T(8,128)} %bitcast.493, f32[2048,2048]{1,0:T(8,128)} %bitcast.492), kind=kLoop, calls=%fused_computation | loop fusion | flops 25165824 | bytes 100663296 | tf_op jit(solution)/shard_map/concatenate | solution.py:239
  969.0 107.2 %all-reduce.3.cloned.1.call-done = f32[2048,2048]{1,0:T(8,128)} async-done(((f32[2048,2048]{1,0:T(8,128)}), f32[2048,2048]{1,0:T(8,128)}) %all-reduce.3.cloned.1.call-update) | async-done | bytes 16777232 | tf_op jit(solution)/shard_map/psum | solution.py:199
  1076.2 11.8 %copy.162 = f32[2048,2048]{1,0:T(8,128)} copy(f32[2048,2048]{1,0:T(8,128)} %all-reduce.3.cloned.1.call-done) | data formatting | bytes 33554432
  (375 shorter events, 114.2 us)
Async XLA Ops:
  7.2 211.4 %all-gather.16.cloned.1.call-start = ((), (), s32[]{:S(2)}) async-start(), calls=%async_computation.8 | async-start | bytes 17825792 | tf_op jit(solution)/shard_map/all_gather | solution.py:171
  7.9 116.8 %copy-start.27 = (f32[2048]{0:T(1024)}, f32[2048]{0:T(1024)S(1)}, u32[]{:S(2)}) copy-start(f32[2048]{0:T(1024)S(1)} %convert_element_type.234) | copy-start | bytes 24580
  11.0 102.9 %copy-start.61 = (f32[256]{0:T(256)}, f32[256]{0:T(256)S(1)}, u32[]{:S(2)}) copy-start(f32[256]{0:T(256)S(1)} %broadcast_multiply_fusion.20) | copy-start | bytes 3076
  11.0 92.0 %copy-start.63 = (f32[256]{0:T(256)}, f32[256]{0:T(256)S(1)}, u32[]{:S(2)}) copy-start(f32[256]{0:T(256)S(1)} %get-tuple-element.145) | copy-start | bytes 3076
  11.1 113.6 %copy-start.65 = (f32[256]{0:T(256)}, f32[256]{0:T(256)S(1)}, u32[]{:S(2)}) copy-start(f32[256]{0:T(256)S(1)} %get-tuple-element.146) | copy-start | bytes 3076
  11.9 102.1 %copy-start.67 = (f32[256]{0:T(256)}, f32[256]{0:T(256)S(1)}, u32[]{:S(2)}) copy-start(f32[256]{0:T(256)S(1)} %fusion.219) | copy-start | bytes 3076
  11.9 112.8 %copy-start.69 = (f32[256]{0:T(256)}, f32[256]{0:T(256)S(1)}, u32[]{:S(2)}) copy-start(f32[256]{0:T(256)S(1)} %fusion.220) | copy-start | bytes 3076
  13.3 89.7 %copy-start.71 = (f32[256]{0:T(256)}, f32[256]{0:T(256)S(1)}, u32[]{:S(2)}) copy-start(f32[256]{0:T(256)S(1)} %fusion.221) | copy-start | bytes 3076
  15.5 219.4 %all-gather.14.cloned.1.call-start = ((), (), s32[]{:S(2)}) async-start(), calls=%async_computation.7 | async-start | bytes 17825792 | tf_op jit(solution)/shard_map/all_gather | solution.py:171
  16.2 296.9 %all-gather.12.cloned.1.call-start = ((), (), s32[]{:S(2)}) async-start(), calls=%async_computation.6 | async-start | bytes 17825792 | tf_op jit(solution)/shard_map/all_gather | solution.py:171
  24.0 139.1 %all-to-all-start.4 = ((bf16[16,256,128]{1,2,0:T(8,128)(2,1)}), bf16[16,256,128]{1,2,0:T(8,128)(2,1)S(1)}, u32[]{:S(2)}, u32[]{:S(2)}) async-start(bf16[16,256,128]{1,2,0:T(8,128)(2,1)} %fusion.162), calls=%async_computation.4 | async-start | bytes 2097152 | tf_op jit(solution)/shard_map/all_to_all | solution.py:176
  80.9 54.5 %copy-start.1 = (f32[256,16,128]{2,0,1:T(8,128)}, f32[256,16,128]{2,0,1:T(8,128)S(1)}, u32[]{:S(2)}) copy-start(f32[256,16,128]{2,0,1:T(8,128)S(1)} %copy.88) | copy-start | bytes 6291460
  141.4 54.3 %copy-start.23 = (f32[16,128]{1,0:T(8,128)}, f32[16,128]{1,0:T(8,128)S(1)}, u32[]{:S(2)}) copy-start(f32[16,128]{1,0:T(8,128)S(1)} %convert_element_type.242) | copy-start | bytes 24580
  141.5 54.3 %copy-start.25 = (f32[16,128]{1,0:T(8,128)}, f32[16,128]{1,0:T(8,128)S(1)}, u32[]{:S(2)}) copy-start(f32[16,128]{1,0:T(8,128)S(1)} %convert_element_type.244) | copy-start | bytes 24580
  163.1 30.2 %all-to-all-start.2 = ((bf16[16,256,128]{1,2,0:T(8,128)(2,1)}), bf16[16,256,128]{1,2,0:T(8,128)(2,1)S(1)}, u32[]{:S(2)}, u32[]{:S(2)}) async-start(bf16[16,256,128]{1,2,0:T(8,128)(2,1)} %fusion.161), calls=%async_computation.2 | async-start | bytes 2097152 | tf_op jit(solution)/shard_map/all_to_all | solution.py:176
  193.3 23.9 %all-to-all-start = ((bf16[16,256,128]{1,2,0:T(8,128)(2,1)}), bf16[16,256,128]{1,2,0:T(8,128)(2,1)S(1)}, u32[]{:S(2)}, u32[]{:S(2)}) async-start(bf16[16,256,128]{1,2,0:T(8,128)(2,1)} %fusion.160), calls=%async_computation | async-start | bytes 2097152 | tf_op jit(solution)/shard_map/all_to_all | solution.py:176
  195.7 704.6 %all-gather.22.cloned.1.call-start = ((), (), s32[]{:S(2)}) async-start(), calls=%async_computation.12 | async-start | bytes 17825792 | tf_op jit(solution)/shard_map/all_gather | solution.py:229
  195.8 130.9 %copy-start.103 = (f32[128]{0:T(128)}, f32[128]{0:T(128)S(1)}, u32[]{:S(2)}) copy-start(f32[128]{0:T(128)S(1)} %get-tuple-element.144) | copy-start | bytes 1540
  195.8 130.9 %copy-start.105 = (f32[128]{0:T(128)}, f32[128]{0:T(128)S(1)}, u32[]{:S(2)}) copy-start(f32[128]{0:T(128)S(1)} %get-tuple-element.143) | copy-start | bytes 1540
  196.0 53.0 %copy-start.29 = (f32[1,1,4096]{2,1,0:T(1,128)}, f32[1,1,4096]{2,1,0:T(1,128)S(1)}, u32[]{:S(2)}) copy-start(f32[1,1,4096]{2,1,0:T(1,128)S(1)} %get-tuple-element.115) | copy-start | bytes 49156
  196.0 53.0 %copy-start.31 = (f32[1,1,4096]{2,1,0:T(1,128)}, f32[1,1,4096]{2,1,0:T(1,128)S(1)}, u32[]{:S(2)}) copy-start(f32[1,1,4096]{2,1,0:T(1,128)S(1)} %get-tuple-element.116) | copy-start | bytes 49156
  196.0 52.9 %copy-start.33 = (f32[1,1,4096]{2,1,0:T(1,128)}, f32[1,1,4096]{2,1,0:T(1,128)S(1)}, u32[]{:S(2)}) copy-start(f32[1,1,4096]{2,1,0:T(1,128)S(1)} %get-tuple-element.117) | copy-start | bytes 49156
  196.0 52.9 %copy-start.35 = (f32[1,1,4096]{2,1,0:T(1,128)}, f32[1,1,4096]{2,1,0:T(1,128)S(1)}, u32[]{:S(2)}) copy-start(f32[1,1,4096]{2,1,0:T(1,128)S(1)} %get-tuple-element.118) | copy-start | bytes 49156
  476.3 66.8 %copy-start.9 = (bf16[16,4,256,128]{3,2,1,0:T(8,128)(2,1)S(1)}, bf16[16,4,256,128]{3,2,1,0:T(8,128)(2,1)}, u32[]{:S(2)}) copy-start(bf16[16,4,256,128]{3,2,1,0:T(8,128)(2,1)} %attn_fwd_bwd.5) | copy-start | bytes 12582916
  622.9 57.1 %all-to-all-start.1 = ((bf16[16,4,256,128]{3,2,1,0:T(8,128)(2,1)}), bf16[16,4,256,128]{3,2,1,0:T(8,128)(2,1)}, u32[]{:S(2)}, u32[]{:S(2)}) async-start(bf16[16,4,256,128]{3,2,1,0:T(8,128)(2,1)} %attn_fwd_bwd.3), calls=%async_computation.1 | async-start | bytes 8388608 | tf_op jit(solution)/shard_map/all_to_all | solution.py:196
  626.4 53.7 %copy-start.42 = (f32[256]{0:T(256)S(1)}, f32[256]{0:T(256)}, u32[]{:S(2)}) copy-start(f32[256]{0:T(256)} %copy-done.41) | copy-start | bytes 3076
  626.4 53.7 %copy-start.44 = (f32[256]{0:T(256)S(1)}, f32[256]{0:T(256)}, u32[]{:S(2)}) copy-start(f32[256]{0:T(256)} %copy-done.43) | copy-start | bytes 3076
  626.4 53.7 %copy-start.46 = (f32[256]{0:T(256)S(1)}, f32[256]{0:T(256)}, u32[]{:S(2)}) copy-start(f32[256]{0:T(256)} %copy-done.45) | copy-start | bytes 3076
  626.4 53.7 %copy-start.48 = (f32[256]{0:T(256)S(1)}, f32[256]{0:T(256)}, u32[]{:S(2)}) copy-start(f32[256]{0:T(256)} %copy-done.47) | copy-start | bytes 3076
  626.4 53.7 %copy-start.54 = (f32[256]{0:T(256)S(1)}, f32[256]{0:T(256)}, u32[]{:S(2)}) copy-start(f32[256]{0:T(256)} %copy-done.53) | copy-start | bytes 3076
  626.5 53.7 %copy-start.56 = (f32[256]{0:T(256)S(1)}, f32[256]{0:T(256)}, u32[]{:S(2)}) copy-start(f32[256]{0:T(256)} %copy-done.55) | copy-start | bytes 3076
  626.5 53.7 %copy-start.58 = (f32[256]{0:T(256)S(1)}, f32[256]{0:T(256)}, u32[]{:S(2)}) copy-start(f32[256]{0:T(256)} %copy-done.57) | copy-start | bytes 3076
  626.5 53.7 %copy-start.60 = (f32[256]{0:T(256)S(1)}, f32[256]{0:T(256)}, u32[]{:S(2)}) copy-start(f32[256]{0:T(256)} %copy-done.59) | copy-start | bytes 3076
  626.5 285.7 %all-gather.18.cloned.1.call-start = ((), (), s32[]{:S(2)}) async-start(), calls=%async_computation.10 | async-start | bytes 17825792 | tf_op jit(solution)/shard_map/all_gather | solution.py:229
  630.0 56.6 %copy-start.79 = (f32[256]{0:T(256)}, f32[256]{0:T(256)S(1)}, u32[]{:S(2)}) copy-start(f32[256]{0:T(256)S(1)} %broadcast_multiply_fusion) | copy-start | bytes 3076
  630.0 56.6 %copy-start.81 = (f32[256]{0:T(256)}, f32[256]{0:T(256)S(1)}, u32[]{:S(2)}) copy-start(f32[256]{0:T(256)S(1)} %broadcast_multiply_fusion.1) | copy-start | bytes 3076
  630.0 56.6 %copy-start.83 = (f32[256]{0:T(256)}, f32[256]{0:T(256)S(1)}, u32[]{:S(2)}) copy-start(f32[256]{0:T(256)S(1)} %broadcast_multiply_fusion.3) | copy-start | bytes 3076
  630.1 56.6 %copy-start.85 = (f32[256]{0:T(256)}, f32[256]{0:T(256)S(1)}, u32[]{:S(2)}) copy-start(f32[256]{0:T(256)S(1)} %broadcast_multiply_fusion.2) | copy-start | bytes 3076
  702.5 23.6 %slice-start.6 = ((s8[16777216]{0:T(1024)(128)(4,1)}), s8[4194304]{0:T(1024)(128)(4,1)S(1)}, s32[]{:S(2)}) async-start(s8[16777216]{0:T(1024)(128)(4,1)} %bitcast.591), calls=%async_computation.19 | async-start | bytes 8388608
  702.5 23.6 %slice-start.7 = ((s8[16777216]{0:T(1024)(128)(4,1)}), s8[4194304]{0:T(1024)(128)(4,1)S(1)}, s32[]{:S(2)}) async-start(s8[16777216]{0:T(1024)(128)(4,1)} %bitcast.591), calls=%async_computation.20 | async-start | bytes 8388608
  735.8 188.2 %all-gather.20.cloned.1.call-start = ((), (), s32[]{:S(2)}) async-start(), calls=%async_computation.11 | async-start | bytes 17825792 | tf_op jit(solution)/shard_map/all_gather | solution.py:229
  735.9 24.0 %slice-start.10 = ((s8[16777216]{0:T(1024)(128)(4,1)}), s8[4194304]{0:T(1024)(128)(4,1)S(1)}, s32[]{:S(2)}) async-start(s8[16777216]{0:T(1024)(128)(4,1)} %bitcast.593), calls=%async_computation.23 | async-start | bytes 8388608
  735.9 24.0 %slice-start.11 = ((s8[16777216]{0:T(1024)(128)(4,1)}), s8[4194304]{0:T(1024)(128)(4,1)S(1)}, s32[]{:S(2)}) async-start(s8[16777216]{0:T(1024)(128)(4,1)} %bitcast.593), calls=%async_computation.24 | async-start | bytes 8388608
  770.3 305.8 %all-reduce.3.cloned.1.call-start = ((), (), s32[]{:S(2)}) async-start(), calls=%async_computation.9 | async-start | bytes 33554432 | tf_op jit(solution)/shard_map/psum | solution.py:199
  828.9 47.3 %copy-start.78 = (f32[256]{0:T(256)S(1)}, f32[256]{0:T(256)}, u32[]{:S(2)}) copy-start(f32[256]{0:T(256)} %copy-done.77) | copy-start | bytes 3076
  828.9 47.3 %copy-start.76 = (f32[256]{0:T(256)S(1)}, f32[256]{0:T(256)}, u32[]{:S(2)}) copy-start(f32[256]{0:T(256)} %copy-done.75) | copy-start | bytes 3076
  828.9 47.4 %copy-start.74 = (f32[256]{0:T(256)S(1)}, f32[256]{0:T(256)}, u32[]{:S(2)}) copy-start(f32[256]{0:T(256)} %copy-done.73) | copy-start | bytes 3076
  828.9 47.4 %copy-start.17 = (bf16[256,2048]{1,0:T(8,128)(2,1)S(1)}, bf16[256,2048]{1,0:T(8,128)(2,1)}, u32[]{:S(2)}) copy-start(bf16[256,2048]{1,0:T(8,128)(2,1)} %fusion.80) | copy-start | bytes 3145732
  (88 other events, 592.7 us)
Sparse Core Ops, SparseCore 0:
  15.6 88.9 all-gather.15
  106.8 87.1 all-gather.13
  196.3 80.7 all-gather.11
  476.4 150.7 all-gather.21
  736.0 75.1 all-gather.17
  813.3 77.5 all-gather.19
  896.3 179.8 all-reduce.2

commit v2 on v1

v2 whole, which is shorter than its diff:
```python
import functools, math
import jax
import jax.numpy as jnp
from jax import lax
from jax.experimental import pallas as pl
from jax.experimental.pallas import tpu as pltpu
from jax.sharding import PartitionSpec as P

def flip(me, off, n_dev):
    res, bit = 0, 1
    while bit < n_dev:
        res = res + lax.rem(me // bit + off // bit % 2, 2) * bit
        bit *= 2
    return res


def meet(n_dev, bits):
    me = lax.axis_index('sp')
    barrier = pltpu.get_barrier_semaphore()
    for bit in bits:
        pl.semaphore_signal(barrier, inc=1, device_id=(flip(me, bit, n_dev),), device_id_type=pl.DeviceIdType.MESH)
    pl.semaphore_wait(barrier, len(bits))


def span(bits):
    res = [0]
    for bit in bits:
        res = res + [off ^ bit for off in res]
    return res


def reduce_plan(n_dev):
    dims = []
    bit = 2
    while bit < n_dev:
        dims.append(bit)
        bit *= 2
    return [[1] + dims[c:] + dims[:c] for c in range(len(dims))]


def scatter_kernel(n_dev, part_ref, dst_ref, acc_ref, recv_ref, rs_send, rs_recv, loc_sem, out_sem):
    me = lax.axis_index('sp')
    rows = part_ref.shape[1]
    orders = reduce_plan(n_dev)
    n_col = len(orders)
    lanes = part_ref.shape[2] // 128
    cuts = [lanes * c // n_col * 128 for c in range(n_col + 1)]
    ids = {}
    for c, order in enumerate(orders):
        for t in range(len(order)):
            for off in span(order[t + 1:]):
                ids[(c, t, off)] = len(ids)

    def block(off):
        return flip(me, off, n_dev) // 2

    def load(off):
        d = flip(me, off, n_dev)
        return pltpu.make_async_copy(part_ref.at[d], acc_ref.at[d // 2], loc_sem.at[off // 2])

    def copy(key):
        c, t, off = key
        bit = orders[c][t]
        cols = pl.ds(cuts[c], cuts[c + 1] - cuts[c])
        k = ids[key]
        src = part_ref.at[flip(me, bit ^ off, n_dev), :, cols] if t == 0 else acc_ref.at[block(bit ^ off), :, cols]
        return pltpu.make_async_remote_copy(src_ref=src, dst_ref=recv_ref.at[k, :, pl.ds(0, cuts[c + 1] - cuts[c])],
                                            send_sem=rs_send.at[k], recv_sem=rs_recv.at[k], device_id=(flip(me, bit, n_dev),), device_id_type=pl.DeviceIdType.MESH)

    def add(key):
        c, t, off = key
        copy(key).wait_recv()
        cols = pl.ds(cuts[c], cuts[c + 1] - cuts[c])
        acc_ref[block(off), :, cols] = acc_ref[block(off), :, cols] + recv_ref[ids[key], :, 0:cuts[c + 1] - cuts[c]]

    bits = [1]
    while bits[-1] * 2 < n_dev:
        bits.append(bits[-1] * 2)
    for off in range(0, n_dev, 2):
        load(off).start()
    meet(n_dev, bits)
    n_step = len(orders[0])
    for t in range(n_step):
        if t == 0:
            for c in range(n_col):
                for off in span(orders[c][1:]):
                    copy((c, 0, off)).start()
            for off in range(0, n_dev, 2):
                load(off).wait()
            continue
        for c in range(n_col):
            bit = orders[c][t]
            for off in span(orders[c][t + 1:]):
                add((c, t - 1, off ^ bit))
                copy((c, t, off)).start()
        for c in range(n_col):
            for off in span(orders[c][t + 1:]):
                add((c, t - 1, off))
    for c in range(n_col):
        add((c, n_step - 1, 0))

    def own(j):
        return pltpu.make_async_copy(acc_ref.at[block(0), :, pl.ds(j * 128, 128)], dst_ref.at[j], out_sem.at[j])

    for j in range(lanes):
        own(j).start()
    for key in ids:
        copy(key).wait_send()
    for j in range(lanes):
        own(j).wait()


def reduce_scatter(part, n_dev, call_id):
    n_row, n_col = part.shape
    rows = n_row // n_dev
    orders = reduce_plan(n_dev)
    n = sum(len(span(order[t + 1:])) for order in orders for t in range(len(order)))
    width = (n_col // 128 + len(orders) - 1) // len(orders) * 128
    sems = pltpu.SemaphoreType.DMA((n,))
    return pl.pallas_call(
        functools.partial(scatter_kernel, n_dev),
        out_shape=jax.ShapeDtypeStruct((n_col // 128, rows, 128), part.dtype),
        in_specs=[pl.BlockSpec(memory_space=pl.ANY)],
        out_specs=pl.BlockSpec(memory_space=pl.ANY),
        scratch_shapes=[pltpu.VMEM((n_dev // 2, rows, n_col), part.dtype), pltpu.VMEM((n, rows, width), part.dtype), sems, sems, pltpu.SemaphoreType.DMA((n_dev // 2,)), pltpu.SemaphoreType.DMA((n_col // 128,))],
        compiler_params=pltpu.CompilerParams(collective_id=call_id, has_side_effects=True, vmem_limit_bytes=32 * 2 ** 20),
        cost_estimate=pl.CostEstimate(flops=10 ** 7, bytes_accessed=part.size * 8, transcendentals=0),
        name="sum_scatter",
    )(part.reshape(n_dev, rows, n_col))


def attn_kernel(blk, tok, n_dev, n_src, slope_ref, q_ref, k_ref, v_ref, do_ref, *refs):
    src_refs, out_ref, dst_refs = refs[:n_src], refs[n_src], refs[n_src + 1:2 * n_src + 1]
    kt_ref, vt_ref, s_ref, dp_ref, dk_ref, dv_ref, acc_ref, send_sem, recv_sem, loc_sem = refs[2 * n_src + 1:]
    i = pl.program_id(0)
    n_blk = pl.num_programs(0)
    me = lax.axis_index('sp')

    def send(j, off):
        peer = flip(me, off, n_dev)
        return pltpu.make_async_remote_copy(src_ref=src_refs[j].at[peer], dst_ref=dst_refs[j].at[me], send_sem=send_sem.at[j, off], recv_sem=recv_sem.at[j, off], device_id=(peer,), device_id_type=pl.DeviceIdType.MESH)

    def keep(j):
        return pltpu.make_async_copy(src_refs[j].at[me], dst_refs[j].at[me], loc_sem.at[j])

    @pl.when(i == 0)
    def _():
        barrier = pltpu.get_barrier_semaphore()
        for off in range(1, n_dev):
            pl.semaphore_signal(barrier, inc=1, device_id=(flip(me, off, n_dev),), device_id_type=pl.DeviceIdType.MESH)
        pl.semaphore_wait(barrier, n_dev - 1)
        for j in range(n_src):
            for off in range(1, n_dev):
                send(j, off).start()
            keep(j).start()

    head_dim = q_ref.shape[1]
    f32, bf16 = jnp.float32, jnp.bfloat16
    scale = head_dim ** -0.5
    log2e = math.log2(math.e)
    slope2 = slope_ref[0] * log2e
    nt = (((1,), (1,)), ((), ()))

    def rows(j):
        return pl.ds(pl.multiple_of(j * blk, blk), blk)

    @pl.when(i == 0)
    def _():
        def fill(j, c):
            sl = rows(j)
            kt_ref[:, sl] = k_ref[sl, :].T
            vt_ref[:, sl] = v_ref[sl, :].T
            dk_ref[sl, :] = jnp.zeros((blk, head_dim), f32)
            dv_ref[sl, :] = jnp.zeros((blk, head_dim), f32)
            return c
        lax.fori_loop(0, n_blk, fill, 0)

    q = q_ref[...]
    do = do_ref[...]

    def lanes(col):
        return jnp.concatenate([col] * (blk // col.shape[1]), axis=1)

    def pass_a(j, mx, diag):
        sl = rows(j)
        s = lax.dot_general(k_ref[sl, :], q, nt, preferred_element_type=f32)
        row = lax.broadcasted_iota(jnp.int32, (blk, 128), 0)
        gap = (row + (j - i) * blk).astype(f32) * slope2
        s = s * (scale * log2e) + lanes(gap)
        if diag:
            key = lax.broadcasted_iota(jnp.int32, (blk, blk), 0)
            qry = lax.broadcasted_iota(jnp.int32, (blk, blk), 1)
            s = jnp.where(key <= qry, s, -1e30)
        s_ref[sl, :] = s
        dp_ref[sl, :] = lax.dot_general(v_ref[sl, :], do, nt, preferred_element_type=f32)
        return jnp.maximum(mx, jnp.max(s.reshape(blk // 8, 8, blk), axis=0))

    mx = lax.fori_loop(0, i, lambda j, c: pass_a(j, c, False), jnp.full((8, blk), -1e30, f32))
    mx = pass_a(i, mx, True)
    mx = jnp.max(mx, axis=0, keepdims=True)

    acc_ref[...] = jnp.zeros(acc_ref.shape, f32)

    def pass_b(j, c):
        tot, dlt = c
        sl = rows(j)
        p = jnp.exp2(s_ref[sl, :] - mx)
        s_ref[sl, :] = p
        acc_ref[...] += jnp.dot(vt_ref[:, sl], p.astype(bf16), preferred_element_type=f32)
        tot = tot + jnp.sum(p.reshape(blk // 8, 8, blk), axis=0)
        dlt = dlt + jnp.sum((p * dp_ref[sl, :]).reshape(blk // 8, 8, blk), axis=0)
        return tot, dlt

    zero = jnp.zeros((8, blk), f32)
    tot, dlt = lax.fori_loop(0, i + 1, pass_b, (zero, zero))
    inv = 1.0 / jnp.sum(tot, axis=0, keepdims=True)
    dlt = jnp.sum(dlt, axis=0, keepdims=True) * inv
    n_tok = blk // tok
    o_blk = (acc_ref[...] * inv).T.astype(bf16)
    for t in range(n_tok):
        out_ref[i * n_tok + t, 0] = o_blk[t * tok:(t + 1) * tok]

    acc_ref[...] = jnp.zeros(acc_ref.shape, f32)

    def pass_c(j, c):
        sl = rows(j)
        p = s_ref[sl, :] * inv
        dv_ref[sl, :] += jnp.dot(p.astype(bf16), do, preferred_element_type=f32)
        ds = (p * (dp_ref[sl, :] - dlt)).astype(bf16)
        dk_ref[sl, :] += jnp.dot(ds, q, preferred_element_type=f32)
        acc_ref[...] += jnp.dot(kt_ref[:, sl], ds, preferred_element_type=f32)
        return c

    lax.fori_loop(0, i + 1, pass_c, 0)
    dq_blk = (acc_ref[...] * scale).T.astype(bf16)
    for t in range(n_tok):
        out_ref[i * n_tok + t, 1] = dq_blk[t * tok:(t + 1) * tok]

    @pl.when(i == n_blk - 1)
    def _():
        for t in range(n_blk * n_tok):
            out_ref[t, 2] = (dk_ref[t * tok:(t + 1) * tok, :] * scale).astype(bf16)
            out_ref[t, 3] = dv_ref[t * tok:(t + 1) * tok, :].astype(bf16)
        for j in range(n_src):
            keep(j).wait()
            for off in range(1, n_dev):
                send(j, off).wait()


def attention(q, k, v, do, slope, tok, srcs, call_id, blk=512):
    n_src, n_dev = len(srcs), srcs[0].shape[0]
    hbm = pl.BlockSpec(memory_space=pl.ANY)
    sems = pltpu.SemaphoreType.DMA((n_src, n_dev))
    seq, head_dim = q.shape
    n_blk = seq // blk
    full = pl.BlockSpec((seq, head_dim), lambda i: (0, 0))
    part = pl.BlockSpec((blk, head_dim), lambda i: (i, 0))
    pairs = seq * (seq + blk) // 2
    f32, bf16 = jnp.float32, jnp.bfloat16
    return pl.pallas_call(
        functools.partial(attn_kernel, blk, tok, n_dev, n_src),
        grid=(n_blk,),
        out_shape=[jax.ShapeDtypeStruct((seq // tok, 4, tok, head_dim), bf16)] + [jax.ShapeDtypeStruct(src.shape, src.dtype) for src in srcs],
        in_specs=[pl.BlockSpec(memory_space=pltpu.SMEM), part, full, full, part] + [hbm] * n_src,
        out_specs=[pl.BlockSpec((seq // tok, 4, tok, head_dim), lambda i: (0, 0, 0, 0))] + [hbm] * n_src,
        scratch_shapes=[
            pltpu.VMEM((head_dim, seq), bf16), pltpu.VMEM((head_dim, seq), bf16),
            pltpu.VMEM((seq, blk), f32), pltpu.VMEM((seq, blk), f32),
            pltpu.VMEM((seq, head_dim), f32), pltpu.VMEM((seq, head_dim), f32),
            pltpu.VMEM((head_dim, blk), f32),
            sems, sems, pltpu.SemaphoreType.DMA((n_src,)),
        ],
        compiler_params=pltpu.CompilerParams(dimension_semantics=("arbitrary",), vmem_limit_bytes=56 * 2 ** 20, collective_id=call_id, has_side_effects=True),
        cost_estimate=pl.CostEstimate(flops=12 * pairs * head_dim * 2, bytes_accessed=8 * seq * head_dim * 2, transcendentals=pairs),
        name="attn_fwd_bwd",
    )(slope, q, k, v, do, *srcs)


def place_kernel(n_grp, width, piece_ref, *refs):
    out_ref = refs[-1]
    n_dev = piece_ref.shape[0]
    for g in range(n_grp):
        for d in range(n_dev):
            out_ref[:, (g * n_dev + d) * width:(g * n_dev + d + 1) * width] = piece_ref[d, :, g * width:(g + 1) * width]


def place(piece, whole, col, n_grp, n_col, rows=256):
    n_dev, n_row, width = piece.shape
    width //= n_grp
    in_specs = [pl.BlockSpec((n_dev, rows, n_grp * width), lambda i: (0, i, 0))]
    args = [piece]
    if whole is not None:
        in_specs.append(pl.BlockSpec(memory_space=pl.ANY))
        args.append(whole)
    return pl.pallas_call(
        functools.partial(place_kernel, n_grp, width),
        grid=(n_row // rows,),
        out_shape=jax.ShapeDtypeStruct((n_row, n_col * n_dev * width), piece.dtype),
        in_specs=in_specs,
        out_specs=pl.BlockSpec((rows, n_grp * n_dev * width), lambda i: (i, col)),
        input_output_aliases={} if whole is None else {1: 0},
        compiler_params=pltpu.CompilerParams(dimension_semantics=("arbitrary",)),
        cost_estimate=pl.CostEstimate(flops=piece.size * 16, bytes_accessed=piece.size * 8, transcendentals=0),
        name="place_cols",
    )(*args)


def rows_kernel(piece_ref, out_ref):
    for j in range(piece_ref.shape[1]):
        out_ref[:, j * 128:(j + 1) * 128] = piece_ref[0, j]


def join_rows(piece):
    n_dev, lanes, rows, _ = piece.shape
    return pl.pallas_call(
        rows_kernel,
        grid=(n_dev,),
        out_shape=jax.ShapeDtypeStruct((n_dev * rows, lanes * 128), piece.dtype),
        in_specs=[pl.BlockSpec((1, lanes, rows, 128), lambda i: (i, 0, 0, 0))],
        out_specs=pl.BlockSpec((rows, lanes * 128), lambda i: (i, 0)),
        compiler_params=pltpu.CompilerParams(dimension_semantics=("arbitrary",)),
        cost_estimate=pl.CostEstimate(flops=piece.size * 16, bytes_accessed=piece.size * 8, transcendentals=0),
        name="join_rows",
    )(piece)


def alibi_slopes(n_heads):
    pow_two = 2 ** math.ceil(math.log2(n_heads))
    exponents = jnp.arange(1, pow_two + 1, dtype=jnp.float32) * (8.0 / pow_two)
    slopes = jnp.exp2(-exponents)
    if pow_two != n_heads:
        slopes = jnp.concatenate([slopes[1::2], slopes[0::2]])[:n_heads]
    return slopes


def layer_norm(values, weight):
    centered = values - jnp.mean(values, axis=-1, keepdims=True)
    var_val = jnp.mean(centered * centered, axis=-1, keepdims=True)
    return centered * lax.rsqrt(var_val + 1e-5) * weight


def row_stats(raw):
    mean = jnp.mean(raw, axis=-1)
    centered = raw - mean[..., None]
    return mean, lax.rsqrt(jnp.mean(centered * centered, axis=-1) + 1e-5)


def solution(mesh):
    n_sp = mesh.shape['sp']
    seq_spec = P(None, 'sp', None)
    rep_spec = P()

    def local_step(x, ln1_w, w_qkv, q_ln_w, k_ln_w, w_out, grad_y):
        f32, bf16 = jnp.float32, jnp.bfloat16
        n_batch, tok, d_model = x.shape
        n_heads, head_dim = q_ln_w.shape
        assert n_heads == n_sp and n_batch == 3
        seq = tok * n_sp
        me = lax.axis_index('sp')
        slope = lax.dynamic_slice_in_dim(alibi_slopes(n_heads), me, 1)
        w_head = jnp.concatenate([lax.dynamic_slice_in_dim(w_qkv, n * d_model + me * head_dim, head_dim, axis=1) for n in range(3)], axis=1)
        ln_flat = [w.reshape(d_model).astype(f32) for w in (q_ln_w, k_ln_w)]
        ln_head = [lax.dynamic_slice_in_dim(w.astype(f32), me, 1, axis=0) for w in (q_ln_w, k_ln_w)]
        x_f32 = x.astype(f32)
        ln1_f32 = ln1_w.astype(f32)

        h_act = layer_norm(x_f32, ln1_f32).astype(bf16)
        h_all = [lax.all_gather(h_act[b], 'sp', axis=0, tiled=True) for b in range(n_batch)]

        d_o = jnp.einsum('bte,fe->btf', grad_y, w_out, preferred_element_type=f32).astype(bf16)
        d_o = jnp.moveaxis(d_o.reshape(n_batch, tok, n_heads, head_dim), 2, 0)
        do_first = lax.all_to_all(d_o[:, 0], 'sp', 0, 0, tiled=True).reshape(seq, head_dim)

        raw_tok = jnp.einsum('bte,ef->btf', h_act, w_qkv[:, :2 * d_model], preferred_element_type=f32)
        stats_tok = [row_stats(raw_tok[..., n * d_model:(n + 1) * d_model]) for n in range(2)]
        stats_all = lax.all_gather(jnp.stack([s for pair in stats_tok for s in pair]), 'sp')
        stats_all = jnp.moveaxis(stats_all, 0, 2).reshape(4, n_batch, seq)

        def grow(b, col):
            return lax.dot_general(h_all[b], col, (((0,), (0,)), ((), ())), preferred_element_type=f32)

        outs, back, xhat = [], [], []
        dv_part, d_head = None, [do_first]
        for b in range(n_batch):
            if b == n_batch - 1:
                dv_part = sum(grow(a, outs[a][:, 3].reshape(seq, head_dim)) for a in range(b))
            if b > 0:
                w_head, outs[-1], dv_part = lax.optimization_barrier((w_head, outs[-1], dv_part))
            raw = jnp.dot(h_all[b], w_head, preferred_element_type=f32)
            hat = [(raw[:, n * head_dim:(n + 1) * head_dim] - stats_all[2 * n, b][:, None]) * stats_all[2 * n + 1, b][:, None] for n in range(2)]
            xhat.append(hat)
            q, k = [(hat[n] * ln_head[n]).astype(bf16) for n in range(2)]
            v = raw[:, 2 * head_dim:].astype(bf16)
            srcs = [d_o[:, a] for a in range(1, n_batch)] if b == 0 else [outs[-1].reshape(n_heads, 4 * tok, head_dim)]
            out, *got = attention(q, k, v, d_head[b], slope, tok, srcs, b)
            if b == 0:
                d_head += [t.reshape(seq, head_dim) for t in got]
            else:
                back.append(got[0].reshape(n_heads, 4, tok, head_dim))
            outs.append(out)
        back.append(lax.all_to_all(outs[-1], 'sp', 0, 0, tiled=True))

        grad_v = dv_part + grow(n_batch - 1, outs[-1][:, 3].reshape(seq, head_dim))
        back[-1], grad_v = lax.optimization_barrier((back[-1], grad_v))
        grad_v = lax.all_gather(grad_v, 'sp')

        def natural(lo, hi):
            return [jnp.stack([jnp.moveaxis(t[:, n], 0, 1).reshape(tok, d_model) for t in back[lo:hi]]) for n in range(4)]

        def token_means(lo, hi, nat):
            res = []
            for n in range(2):
                hat = (raw_tok[lo:hi, :, n * d_model:(n + 1) * d_model] - stats_tok[n][0][lo:hi, :, None]) * stats_tok[n][1][lo:hi, :, None]
                gw = nat[1 + n].astype(f32) * ln_flat[n]
                res += [jnp.mean(gw, axis=-1), jnp.mean(gw * hat, axis=-1)]
            return jnp.stack(res)

        def first_half(lo, hi, nat, mean):
            y = (jnp.einsum('btd,de->bte', nat[0], w_out, preferred_element_type=f32) + x_f32[lo:hi]).astype(bf16)
            stat = [[s[lo:hi, :, None] for s in pair] for pair in stats_tok]
            hats = [(raw_tok[lo:hi, :, n * d_model:(n + 1) * d_model] - stat[n][0]) * stat[n][1] for n in range(2)]
            grads = [nat[1 + n].astype(f32) for n in range(2)]
            raws = [((grads[n] * ln_flat[n] - mean[2 * n][..., None] - hats[n] * mean[2 * n + 1][..., None]) * stat[n][1]).astype(bf16) for n in range(2)]
            d_qkv = jnp.concatenate(raws + [nat[3]], axis=-1)
            d_h = jnp.einsum('bte,de->btd', d_qkv, w_qkv, preferred_element_type=f32).astype(bf16)
            return y, d_h, [jnp.sum(grads[n] * hats[n], axis=(0, 1)) for n in range(2)]

        def second_half(lo, hi, d_h):
            _, ln1_pull = jax.vjp(layer_norm, x_f32[lo:hi], ln1_f32)
            d_x, grad_ln1 = ln1_pull(d_h.astype(f32))
            return (d_x + grad_y[lo:hi].astype(f32)).astype(bf16), grad_ln1

        last = n_batch - 1
        nat_a = natural(0, last)
        mean_a = token_means(0, last, nat_a)
        nat_b = natural(last, n_batch)
        mean_b = token_means(last, n_batch, nat_b)
        means_all = lax.all_gather(jnp.concatenate([mean_a, mean_b], axis=1), 'sp')
        means_all = jnp.moveaxis(means_all, 0, 2).reshape(4, n_batch, seq)

        total = 0.0
        for b in range(n_batch):
            cols = []
            for n in range(2):
                gw = outs[b][:, 1 + n].reshape(seq, head_dim).astype(f32) * ln_head[n]
                rstd = stats_all[2 * n + 1, b][:, None]
                cols.append(((gw - means_all[2 * n, b][:, None] - xhat[b][n] * means_all[2 * n + 1, b][:, None]) * rstd).astype(bf16))
            total = total + grow(b, jnp.concatenate(cols, axis=1))
        total, grad_v = lax.optimization_barrier((total, grad_v))
        grad_qk = lax.all_gather(total, 'sp')

        o_tok = jnp.concatenate([nat_a[0], nat_b[0]])
        w_out_part = jnp.einsum('btd,bte->de', o_tok, grad_y, preferred_element_type=f32)
        w_out_part, total = lax.optimization_barrier((w_out_part, total))
        w_out_sum = reduce_scatter(w_out_part, n_sp, n_batch)
        nat = [jnp.concatenate(pair) for pair in zip(nat_a, nat_b)]
        mean = jnp.concatenate([mean_a, mean_b], axis=1)
        w_out_sum, nat, mean = lax.optimization_barrier((w_out_sum, nat, mean))
        y, d_h, ln_grads = first_half(0, n_batch, nat, mean)
        w_out_sum, grad_qk, d_h, y = lax.optimization_barrier((w_out_sum, grad_qk, d_h, y))
        w_out_all = lax.all_gather(w_out_sum, 'sp')
        grad_x, grad_ln1 = second_half(0, n_batch, d_h)
        small = jnp.sum(lax.all_gather(jnp.stack([grad_ln1] + ln_grads), 'sp'), axis=0)
        grad_w_qkv = place(grad_v, None, 2, 1, 3)
        grad_w_qkv = place(grad_qk, grad_w_qkv, 0, 2, 3)
        grad_w_out = join_rows(w_out_all)
        return (y, grad_x, small[0], grad_w_qkv, small[1].reshape(n_heads, head_dim), small[2].reshape(n_heads, head_dim), grad_w_out)

    return jax.shard_map(local_step, mesh=mesh, in_specs=(seq_spec, rep_spec, rep_spec, rep_spec, rep_spec, rep_spec, seq_spec), out_specs=(seq_spec, seq_spec, rep_spec, rep_spec, rep_spec, rep_spec, rep_spec), check_vma=False)
```

time: 1100 us -> 895 us (0.81)
  Pallas kernels: 167 us -> 383 us
  blocking collectives: 208 us -> 43.9 us
  matrix products: 261 us -> 157 us
  waiting for transfers between devices: 195 us -> 101 us
  local copies, waits for them, and re-layouts: 146 us -> 87.5 us
    pallas_call x3 -> x7, Pallas kernels: 167 us -> 383 us  [the longest x3 212 us: attention(): pl.pallas_call(functools.partial(attn_kernel, blk, tok, n_dev, n_src), gr...]
    all_to_all x2 -> x0, blocking collectives: 147 us -> none  [local_step(): back.append(lax.all_to_all(out, 'sp', 0, 0, tiled=True))]
    psum x1 -> x0, waiting for transfers between devices: 107 us -> none  [local_step(): lax.psum(jnp.einsum('bhtd,bte->hde', o_tok, grad_y, preferred_element_typ...]
    all_gather x6, waiting for transfers between devices: 0.01 us -> 57.8 us  [the longest x3 47 us: local_step(): lax.all_gather(h_act[b], 'sp', axis=0, tiled=True)]
    dot_general x19 -> x11, matrix products: 177 us -> 121 us  [the longest x6 46.9 us: grow(): lax.dot_general(h_all[b], col, (((0,), (0,)), ((), ())), preferred_elemen...]
    unnamed x6 -> x0, matrix products: 46.9 us -> none
    all_to_all x4 -> x2, waiting for transfers between devices: 86 us -> 41.7 us  [the longest x1 41.7 us: local_step(): back.append(lax.all_to_all(outs[-1], 'sp', 0, 0, tiled=True))]
    unnamed x252 -> x156, local copies, waits for them, and re-layouts: 55.4 us -> 17.9 us
  transfers between devices with their start and end apart: 11 -> 8, of which waited for: 4 -> 5; matrix products, arithmetic and copies ran while one was open for 38% -> 33% of each run, Pallas kernels for 5% -> 34%
where the time goes in v2:
time: 895 us; the launch traced here: 885 us
  Pallas kernels  383 us (43%)
  matrix products  157 us (18%)
  waiting for transfers between devices  101 us (11%)
  local copies, waits for them, and re-layouts  87.5 us (10%)
  other arithmetic  87.4 us (10%)
  blocking collectives  43.9 us (5%)
  between operations  15.7 us (2%)
    pallas_call x3, Pallas kernels, attention(): pl.pallas_call(functools.partial(attn_kernel, blk, tok, n_dev, n_src), gr...  212 us
    pallas_call x1, Pallas kernels, reduce_scatter(): pl.pallas_call(functools.partial(scatter_kernel, n_dev), out_shape=jax.Sh...  116 us
    all_gather x3, waiting for transfers between devices, local_step(): lax.all_gather(h_act[b], 'sp', axis=0, tiled=True)  47 us
    dot_general x6, matrix products, grow(): lax.dot_general(h_all[b], col, (((0,), (0,)), ((), ())), preferred_elemen...  46.9 us
    all_to_all x1, waiting for transfers between devices, local_step(): back.append(lax.all_to_all(outs[-1], 'sp', 0, 0, tiled=True))  41.7 us
    pallas_call x2, Pallas kernels, place(): pl.pallas_call(functools.partial(place_kernel, n_grp, width), grid=(n_row...  37.6 us
    dot_general x3, matrix products, local_step(): raw = jnp.dot(h_all[b], w_head, preferred_element_type=f32)  36.3 us
    transpose x15, local copies, waits for them, and re-layouts, natural(): jnp.moveaxis(t[:, n], 0, 1).reshape(tok, d_model)  31.9 us
  transfers between devices with their start and end apart: 8, of which 5 were waited for; matrix products, arithmetic and copies ran while one was open for 33% of the time, Pallas kernels for 34%

profile of v2, /device:TPU:0, one launch (start us, length us, event | category | flops | bytes accessed | tf_op | source)
XLA Modules:
  0.0 884.7 jit_solution(5798748618090920495)
XLA Ops:
  17.3 10.1 %fusion.64 = bf16[3,256,2048]{2,1,0:T(8,128)(2,1)S(1)} fusion(bf16[3,256,2048]{2,1,0:T(8,128)(2,1)} %param.13, bf16[2048,2048]{1,0:T(8,128)(2,1)} %param.12), kind=kOutput, calls=%fused_computation.84 | convolution fusion | flops 6444023808 | bytes 14680064 | tf_op jit(solution)/shard_map/bte,fe->btf/dot_general | solution.py:370
  30.2 3.5 copy.102
  35.5 5.3 all-to-all-start
  40.8 16.9 %fusion.8 = f32[3,256,4096]{2,1,0:T(8,128)S(1)} fusion(bf16[3,256,2048]{2,1,0:T(8,128)(2,1)} %copy-done.8, bf16[2048,6144]{1,0:T(8,128)(2,1)} %param.9), kind=kOutput, calls=%fused_computation.8 | convolution fusion | flops 12884901888 | bytes 32505856 | tf_op jit(solution)/shard_map/bte,ef->btf/dot_general | solution.py:374
  58.4 4.1 copy-done.1
  65.3 14.5 %all-gather.2 = f32[64,3,256]{2,1,0:T(4,128)S(1)} all-gather(f32[4,3,256]{2,1,0:T(4,128)S(1)} %pad_maximum_fusion.7), channel_id=4, replica_groups=mesh['sp'=16] {'sp'}, dimensions={0}, use_global_device_ids=true | all-gather | bytes 208896 | tf_op jit(solution)/shard_map/all_gather | solution.py:376
  84.1 22.8 %all-gather.19.cloned.1.call-done = bf16[1,4096,2048]{2,1,0:T(8,128)(2,1)} async-done(((bf16[1,256,2048]{2,1,0:T(8,128)(2,1)}), bf16[1,4096,2048]{2,1,0:T(8,128)(2,1)}) %all-gather.19.cloned.1.call-update) | async-done | bytes 16777232 | tf_op jit(solution)/shard_map/all_gather | solution.py:368
  107.0 12.2 %fusion.14 = f32[4096,384]{1,0:T(8,128)S(1)} fusion(bf16[1,4096,2048]{2,1,0:T(8,128)(2,1)} %all-gather.19.cloned.1.call-done, bf16[2048,128]{1,0:T(8,128)(2,1)S(1)} %get-tuple-element.78, bf16[2048,128]{1,0:T(8,128)(2,1)S(1)} %get-tuple-element.79, bf16[2048,128]{1,0:T(8,128)(2,1)S(1)} %get-tuple-element.77), kind=kOutput, calls=%fused_computation.14 | convolution fusion | flops 6447169536 | bytes 24641536 | tf_op jit(solution)/shard_map/dot_general | solution.py:389
  122.3 4.2 multiply_convert_fusion.4
  126.5 58.8 %attn_fwd_bwd.3 = (bf16[16,4,256,128]{3,2,1,0:T(8,128)(2,1)}, bf16[16,256,128]{2,1,0:T(8,128)(2,1)}, bf16[16,256,128]{2,1,0:T(8,128)(2,1)}) custom-call(f32[1]{0:T(128)} %dynamic_slice.18.slope_ref, bf16[4096,128]{1,0:T(8,128)(2,1)} %get-tuple-element.93.q_ref, bf16[4096,128]{1,0:T(8,128)(2,1)} %get-tuple-element.92.k_ref, bf16[4096,128]{1,0:T(8,128)(2,1)} %slice.521.v_ref, ...), custom_call_target="tpu_custom_call" | custom-call | flops 28991029248 | bytes 8388608 | tf_op jit(solution)/shard_map/attn_fwd_bwd/pallas_call | solution.py:260
  185.3 22.3 %all-gather.17.cloned.1.call-done = bf16[1,4096,2048]{2,1,0:T(8,128)(2,1)} async-done(((bf16[1,256,2048]{2,1,0:T(8,128)(2,1)}), bf16[1,4096,2048]{2,1,0:T(8,128)(2,1)}) %all-gather.17.cloned.1.call-update) | async-done | bytes 16777232 | tf_op jit(solution)/shard_map/all_gather | solution.py:368
  207.6 12.0 %fusion.20 = f32[4096,384]{1,0:T(8,128)S(1)} fusion(bf16[2048,384]{1,0:T(8,128)(2,1)S(1)} %pad_maximum_fusion.6, bf16[1,4096,2048]{2,1,0:T(8,128)(2,1)} %all-gather.17.cloned.1.call-done), kind=kOutput, calls=%fused_computation.20 | convolution fusion | flops 6442450944 | bytes 24641536 | tf_op jit(solution)/shard_map/dot_general | solution.py:389
  220.9 4.8 multiply_convert_fusion.2
  225.7 89.8 %attn_fwd_bwd.4 = (bf16[16,4,256,128]{3,2,1,0:T(8,128)(2,1)}, bf16[16,1024,128]{2,1,0:T(8,128)(2,1)}) custom-call(f32[1]{0:T(128)} %dynamic_slice.18.slope_ref, bf16[4096,128]{1,0:T(8,128)(2,1)} %get-tuple-element.91.q_ref, bf16[4096,128]{1,0:T(8,128)(2,1)} %get-tuple-element.90.k_ref, bf16[4096,128]{1,0:T(8,128)(2,1)} %slice.520.v_ref, ...), custom_call_target="tpu_custom_call" | custom-call | flops 28991029248 | bytes 8388608 | tf_op jit(solution)/shard_map/attn_fwd_bwd/pallas_call | solution.py:260
  318.7 9.0 %fusion.12 = f32[2048,128]{1,0:T(8,128)S(1)} fusion(bf16[4096,128]{1,0:T(8,128)(2,1)S(1)} %bitcast.263, bf16[1,4096,2048]{2,1,0:T(8,128)(2,1)} %all-gather.19.cloned.1.call-done), kind=kOutput, calls=%fused_computation.12 | convolution fusion | flops 2147483648 | bytes 18874368 | tf_op jit(solution)/shard_map/dot_general | solution.py:380
  327.7 4.8 fusion.78
  334.4 12.0 %fusion.6 = f32[4096,384]{1,0:T(8,128)S(1)} fusion(bf16[2048,384]{1,0:T(8,128)(2,1)S(1)} %pad_maximum_fusion.6, bf16[1,4096,2048]{2,1,0:T(8,128)(2,1)} %all-gather.21.cloned.1.call-done), kind=kOutput, calls=%fused_computation.6 | convolution fusion | flops 6442450944 | bytes 24641536 | tf_op jit(solution)/shard_map/dot_general | solution.py:389
  347.6 4.9 multiply_convert_fusion
  352.5 63.8 %attn_fwd_bwd.5 = (bf16[16,4,256,128]{3,2,1,0:T(8,128)(2,1)}, bf16[16,1024,128]{2,1,0:T(8,128)(2,1)}) custom-call(f32[1]{0:T(128)} %dynamic_slice.18.slope_ref, bf16[4096,128]{1,0:T(8,128)(2,1)} %get-tuple-element.89.q_ref, bf16[4096,128]{1,0:T(8,128)(2,1)} %get-tuple-element.88.k_ref, bf16[4096,128]{1,0:T(8,128)(2,1)} %slice.519.v_ref, ...), custom_call_target="tpu_custom_call" | custom-call | flops 28991029248 | bytes 8388608 | tf_op jit(solution)/shard_map/attn_fwd_bwd/pallas_call | solution.py:260
  419.7 3.5 fusion.140
  423.2 9.3 %fusion.81 = f32[2048,128]{1,0:T(8,128)} fusion(f32[2048,128]{1,0:T(8,128)S(1)} %fusion.78, bf16[4096,128]{1,0:T(8,128)(2,1)S(1)} %bitcast.264, bf16[1,4096,2048]{2,1,0:T(8,128)(2,1)} %all-gather.21.cloned.1.call-done), kind=kOutput, calls=%fused_computation.93 | convolution fusion | flops 2147745792 | bytes 19922944 | tf_op jit(solution)/shard_map/dot_general | solution.py:380
  432.5 41.7 %all-to-all-done.1 = bf16[16,4,256,128]{3,2,1,0:T(8,128)(2,1)} async-done(((bf16[16,4,256,128]{3,2,1,0:T(8,128)(2,1)}), bf16[16,4,256,128]{3,2,1,0:T(8,128)(2,1)}, u32[]{:S(2)}, u32[]{:S(2)}) %all-to-all-start.1) | async-done | bytes 4194336 | tf_op jit(solution)/shard_map/all_to_all | solution.py:401
  474.4 4.0 slice_bitcast_fusion
  479.8 4.0 slice_bitcast_fusion.1
  495.4 5.0 fusion.58
  501.9 4.0 slice_bitcast_fusion.11
  512.6 3.9 fusion.89
  518.8 15.1 %all-gather.4 = f32[64,3,256]{2,1,0:T(4,128)S(1)} all-gather(f32[4,3,256]{2,1,0:T(4,128)S(1)} %maximum_maximum_fusion), channel_id=6, replica_groups=mesh['sp'=16] {'sp'}, dimensions={0}, use_global_device_ids=true | all-gather | bytes 208896 | tf_op jit(solution)/shard_map/all_gather | solution.py:438
  534.3 5.7 fusion.128
  540.1 5.3 fusion.120
  545.4 5.3 fusion.112
  550.7 8.4 fusion.10
  560.1 5.3 fusion.72
  565.4 10.1 %fusion.75 = f32[2048,256]{1,0:T(8,128)} fusion(f32[2048,256]{1,0:T(8,128)S(1)} %fusion.72, bf16[1,4096,2048]{2,1,0:T(8,128)(2,1)} %all-gather.21.cloned.1.call-done, bf16[4096,128]{1,0:T(8,128)(2,1)S(1)} %get-tuple-element.83, bf16[4096,128]{1,0:T(8,128)(2,1)S(1)} %get-tuple-element.82), kind=kOutput, calls=%fused_computation.91 | convolution fusion | flops 4299685888 | bytes 23068672 | tf_op jit(solution)/shard_map/dot_general | solution.py:380
  588.8 3.4 pad_maximum_fusion.1
  601.2 9.7 %convolution_bitcast_fusion = f32[2048,2048]{1,0:T(8,128)} fusion(bf16[3,256,2048]{2,1,0:T(8,128)(2,1)S(1)} %copy-done.31, bf16[1,256,2048]{1,2,0:T(8,128)(2,1)S(1)} %bitcast.257, bf16[1,256,2048]{1,2,0:T(8,128)(2,1)S(1)} %bitcast.253, bf16[1,256,2048]{1,2,0:T(8,128)(2,1)S(1)} %bitcast.255), kind=kOutput, calls=%fused_computation.36 | convolution fusion | flops 6445596672 | bytes 23068672 | tf_op jit(solution)/shard_map/btd,bte->de/dot_general | solution.py:453
  610.9 5.8 copy-done
  616.7 115.9 %sum_scatter.1 = f32[16,128,128]{2,1,0:T(8,128)} custom-call(f32[16,128,2048]{2,1,0:T(8,128)S(1)} %bitcast.235), custom_call_target="tpu_custom_call" | custom-call | flops 10000000 | bytes 33554432 | tf_op jit(solution)/shard_map/sum_scatter/pallas_call | solution.py:120
  732.6 13.1 %fusion.43 = (f32[2048]{0:T(1024)S(1)}, f32[2048]{0:T(1024)S(1)}, bf16[3,256,2048]{2,1,0:T(8,128)(2,1)}, bf16[3,256,2048]{2,1,0:T(8,128)(2,1)}) fusion(bf16[3,256,2048]{2,1,0:T(8,128)(2,1)} %pad_maximum_fusion.1, f32[3,256,4096]{2,1,0:T(8,128)} %copy-done.1, f32[3,256]{1,0:T(4,128)S(1)} %copy-done.61, f32[3,256]{1,0:T(4,128)S(1)} %copy-done.51, ...), kind=kLoop, calls=%fused_computation.54 | loop fusion | flops 34598912 | bytes 25223168 | tf_op jit(solution)/shard_map/reduce_sum | solution.py:426
  745.7 10.6 %fusion.52 = bf16[3,256,2048]{2,1,0:T(8,128)(2,1)} fusion(bf16[3,256,2048]{2,1,0:T(8,128)(2,1)S(1)} %copy-done.3, bf16[3,256,2048]{1,2,0:T(8,128)(2,1)S(1)} %copy-done.30, bf16[2048,2048]{1,0:T(8,128)(2,1)} %param.12), kind=kOutput, calls=%fused_computation.63 | convolution fusion | flops 6447169536 | bytes 17825792 | tf_op jit(solution)/shard_map/btd,de->bte/dot_general | solution.py:419
  756.4 26.4 %fusion.67 = bf16[3,256,2048]{2,1,0:T(8,128)(2,1)} fusion(bf16[2048,6144]{1,0:T(8,128)(2,1)} %param.9, bf16[3,256,2048]{2,1,0:T(8,128)(2,1)} %pad_maximum_fusion.3, bf16[3,256,2048]{2,1,0:T(8,128)(2,1)} %get-tuple-element.80, bf16[3,256,2048]{2,1,0:T(8,128)(2,1)} %get-tuple-element.81), kind=kOutput, calls=%fused_computation.85 | convolution fusion | flops 19357237248 | bytes 37748736 | tf_op jit(solution)/shard_map/bte,de->btd/dot_general | solution.py:425
  782.8 14.2 %place_cols.2.refs_0_ = f32[2048,6144]{1,0:T(8,128)} custom-call(f32[16,2048,128]{2,1,0:T(8,128)} %bitcast.238), custom_call_target="tpu_custom_call" | custom-call | flops 67108864 | bytes 33554432 | tf_op jit(solution)/shard_map/place_cols/pallas_call | solution.py:295
  797.0 3.4 fusion.51
  803.8 14.3 %all-gather.9 = f32[16,3,2048]{2,1,0:T(4,128)} all-gather(f32[1,3,2048]{2,1,0:T(4,128)S(1)} %maximum_bitcast_fusion), channel_id=9, replica_groups=mesh['sp'=16] {'sp'}, dimensions={0}, use_global_device_ids=true | all-gather | bytes 417792 | tf_op jit(solution)/shard_map/all_gather | solution.py:463
  819.3 23.4 %place_cols.3 = f32[2048,6144]{1,0:T(8,128)} custom-call(f32[16,2048,256]{2,1,0:T(8,128)} %bitcast.236, f32[2048,6144]{1,0:T(8,128)} %place_cols.2.refs_0_), custom_call_target="tpu_custom_call", output_to_operand_aliasing={{}: (1, {})} | custom-call | flops 134217728 | bytes 67108864 | tf_op jit(solution)/shard_map/place_cols/pallas_call | solution.py:295
  843.2 5.8 add_convert_fusion
  849.0 10.8 %all-gather.27.cloned.1.call-done = f32[256,128,128]{2,1,0:T(8,128)} async-done(((f32[16,128,128]{2,1,0:T(8,128)}), f32[256,128,128]{2,1,0:T(8,128)}) %all-gather.27.cloned.1.call-update) | async-done | bytes 16777232 | tf_op jit(solution)/shard_map/all_gather | solution.py:461
  859.9 17.6 %join_rows.1 = f32[2048,2048]{1,0:T(8,128)} custom-call(f32[16,16,128,128]{3,2,1,0:T(8,128)} %bitcast.237), custom_call_target="tpu_custom_call" | custom-call | flops 67108864 | bytes 33554432 | tf_op jit(solution)/shard_map/join_rows/pallas_call | solution.py:315
  (257 shorter events, 88.2 us)
Async XLA Ops:
  7.2 99.8 %all-gather.19.cloned.1.call-start = ((), (), s32[]{:S(2)}) async-start(), calls=%async_computation.3 | async-start | bytes 17825792 | tf_op jit(solution)/shard_map/all_gather | solution.py:368
  15.8 191.8 %all-gather.17.cloned.1.call-start = ((), (), s32[]{:S(2)}) async-start(), calls=%async_computation.2 | async-start | bytes 17825792 | tf_op jit(solution)/shard_map/all_gather | solution.py:368
  16.6 317.8 %all-gather.21.cloned.1.call-start = ((), (), s32[]{:S(2)}) async-start(), calls=%async_computation.4 | async-start | bytes 17825792 | tf_op jit(solution)/shard_map/all_gather | solution.py:368
  35.5 91.0 %all-to-all-start = ((bf16[16,256,128]{2,1,0:T(8,128)(2,1)}), bf16[16,256,128]{2,1,0:T(8,128)(2,1)}, u32[]{:S(2)}, u32[]{:S(2)}) async-start(bf16[16,256,128]{2,1,0:T(8,128)(2,1)} %get-tuple-element.119), calls=%async_computation | async-start | bytes 2097152 | tf_op jit(solution)/shard_map/all_to_all | solution.py:372
  62.5 17.9 %copy-start.62 = (bf16[16,128]{1,0:T(8,128)(2,1)S(1)}, bf16[16,128]{1,0:T(8,128)(2,1)}, u32[]{:S(2)}) copy-start(bf16[16,128]{1,0:T(8,128)(2,1)} %param.10) | copy-start | bytes 12292
  62.5 18.5 %copy-start.63 = (bf16[16,128]{1,0:T(8,128)(2,1)S(1)}, bf16[16,128]{1,0:T(8,128)(2,1)}, u32[]{:S(2)}) copy-start(bf16[16,128]{1,0:T(8,128)(2,1)} %param.11) | copy-start | bytes 12292
  84.1 36.4 %copy-start.38 = (f32[1,1,4096]{2,0,1:T(1,128)}, f32[1,1,4096]{2,0,1:T(1,128)S(1)}, u32[]{:S(2)}) copy-start(f32[1,1,4096]{2,0,1:T(1,128)S(1)} %get-tuple-element.140) | copy-start | bytes 49156
  84.1 36.4 %copy-start.40 = (f32[1,1,4096]{2,0,1:T(1,128)}, f32[1,1,4096]{2,0,1:T(1,128)S(1)}, u32[]{:S(2)}) copy-start(f32[1,1,4096]{2,0,1:T(1,128)S(1)} %get-tuple-element.141) | copy-start | bytes 49156
  84.1 36.3 %copy-start.42 = (f32[1,1,4096]{2,0,1:T(1,128)}, f32[1,1,4096]{2,0,1:T(1,128)S(1)}, u32[]{:S(2)}) copy-start(f32[1,1,4096]{2,0,1:T(1,128)S(1)} %get-tuple-element.142) | copy-start | bytes 49156
  84.1 36.3 %copy-start.44 = (f32[1,1,4096]{2,0,1:T(1,128)}, f32[1,1,4096]{2,0,1:T(1,128)S(1)}, u32[]{:S(2)}) copy-start(f32[1,1,4096]{2,0,1:T(1,128)S(1)} %get-tuple-element.143) | copy-start | bytes 49156
  219.6 6.1 copy-start.6
  225.7 91.3 %copy-start.32 = (bf16[16,4,256,128]{3,2,1,0:T(8,128)(2,1)S(1)}, bf16[16,4,256,128]{3,2,1,0:T(8,128)(2,1)}, u32[]{:S(2)}) copy-start(bf16[16,4,256,128]{3,2,1,0:T(8,128)(2,1)} %get-tuple-element.37) | copy-start | bytes 12582916
  315.5 12.2 %slice-start.6 = ((s8[16777216]{0:T(1024)(128)(4,1)}), s8[4194304]{0:T(1024)(128)(4,1)S(1)}, s32[]{:S(2)}) async-start(s8[16777216]{0:T(1024)(128)(4,1)} %bitcast.317), calls=%async_computation.14 | async-start | bytes 8388608
  317.0 10.7 %slice-start.7 = ((s8[16777216]{0:T(1024)(128)(4,1)}), s8[4194304]{0:T(1024)(128)(4,1)S(1)}, s32[]{:S(2)}) async-start(s8[16777216]{0:T(1024)(128)(4,1)} %bitcast.317), calls=%async_computation.15 | async-start | bytes 8388608
  318.7 9.1 %slice-start.8 = ((s8[16777216]{0:T(1024)(128)(4,1)}), s8[4194304]{0:T(1024)(128)(4,1)S(1)}, s32[]{:S(2)}) async-start(s8[16777216]{0:T(1024)(128)(4,1)} %bitcast.317), calls=%async_computation.16 | async-start | bytes 8388608
  318.7 9.1 %slice-start.9 = ((s8[16777216]{0:T(1024)(128)(4,1)}), s8[4194304]{0:T(1024)(128)(4,1)S(1)}, s32[]{:S(2)}) async-start(s8[16777216]{0:T(1024)(128)(4,1)} %bitcast.317), calls=%async_computation.17 | async-start | bytes 8388608
  346.4 6.1 copy-start.7
  416.3 57.8 %all-to-all-start.1 = ((bf16[16,4,256,128]{3,2,1,0:T(8,128)(2,1)}), bf16[16,4,256,128]{3,2,1,0:T(8,128)(2,1)}, u32[]{:S(2)}, u32[]{:S(2)}) async-start(bf16[16,4,256,128]{3,2,1,0:T(8,128)(2,1)} %get-tuple-element.44), calls=%async_computation.1 | async-start | bytes 8388608 | tf_op jit(solution)/shard_map/all_to_all | solution.py:401
  419.6 155.9 %all-gather.23.cloned.1.call-start = ((), (), s32[]{:S(2)}) async-start(), calls=%async_computation.5 | async-start | bytes 17825792 | tf_op jit(solution)/shard_map/all_gather | solution.py:405
  423.2 51.1 %copy-start.51 = (f32[3,256]{1,0:T(4,128)S(1)}, f32[3,256]{1,0:T(4,128)}, u32[]{:S(2)}) copy-start(f32[3,256]{1,0:T(4,128)} %copy-done.50) | copy-start | bytes 9220
  423.2 51.1 %copy-start.53 = (f32[3,256]{1,0:T(4,128)S(1)}, f32[3,256]{1,0:T(4,128)}, u32[]{:S(2)}) copy-start(f32[3,256]{1,0:T(4,128)} %copy-done.52) | copy-start | bytes 9220
  423.2 51.1 %copy-start.61 = (f32[3,256]{1,0:T(4,128)S(1)}, f32[3,256]{1,0:T(4,128)}, u32[]{:S(2)}) copy-start(f32[3,256]{1,0:T(4,128)} %get-tuple-element.157) | copy-start | bytes 9220
  423.2 51.2 %copy-start.60 = (f32[3,256]{1,0:T(4,128)S(1)}, f32[3,256]{1,0:T(4,128)}, u32[]{:S(2)}) copy-start(f32[3,256]{1,0:T(4,128)} %get-tuple-element.153) | copy-start | bytes 9220
  474.2 308.5 %all-gather.25.cloned.1.call-start = ((), (), s32[]{:S(2)}) async-start(), calls=%async_computation.6 | async-start | bytes 35651584 | tf_op jit(solution)/shard_map/all_gather | solution.py:450
  485.0 10.4 %copy-start.9 = (bf16[1,256,2048]{2,1,0:T(8,128)(2,1)}, bf16[1,256,2048]{2,1,0:T(8,128)(2,1)S(1)}, u32[]{:S(2)}) copy-start(bf16[1,256,2048]{2,1,0:T(8,128)(2,1)S(1)} %stack_reshape.39) | copy-start | bytes 3145732
  488.3 7.1 copy-start.46
  488.3 7.1 copy-start.47
  489.8 10.5 %copy-start.11 = (bf16[1,256,2048]{2,1,0:T(8,128)(2,1)}, bf16[1,256,2048]{2,1,0:T(8,128)(2,1)S(1)}, u32[]{:S(2)}) copy-start(bf16[1,256,2048]{2,1,0:T(8,128)(2,1)S(1)} %stack_reshape.42) | copy-start | bytes 3145732
  510.2 24.0 %slice-start = ((s8[6291456]{0:T(1024)(128)(4,1)}), s8[2097152]{0:T(1024)(128)(4,1)S(1)}, s32[]{:S(2)}) async-start(s8[6291456]{0:T(1024)(128)(4,1)} %bitcast.239), calls=%async_computation.8 | async-start | bytes 4194304
  512.6 21.6 %slice-start.1 = ((s8[6291456]{0:T(1024)(128)(4,1)}), s8[4194304]{0:T(1024)(128)(4,1)S(1)}, s32[]{:S(2)}) async-start(s8[6291456]{0:T(1024)(128)(4,1)} %bitcast.239), calls=%async_computation.9 | async-start | bytes 8388608
  512.6 27.4 %slice-start.2 = ((s8[6291456]{0:T(1024)(128)(4,1)}), s8[2097152]{0:T(1024)(128)(4,1)S(1)}, s32[]{:S(2)}) async-start(s8[6291456]{0:T(1024)(128)(4,1)} %bitcast.241), calls=%async_computation.10 | async-start | bytes 4194304
  516.5 17.7 %copy-start.15 = (bf16[16,1,256,128]{3,2,1,0:T(8,128)(2,1)S(1)}, bf16[16,1,256,128]{3,2,1,0:T(8,128)(2,1)}, u32[]{:S(2)}) copy-start(bf16[16,1,256,128]{3,2,1,0:T(8,128)(2,1)} %get-tuple-element.111) | copy-start | bytes 3145732
  516.5 17.7 %copy-start.16 = (bf16[16,1,256,128]{3,2,1,0:T(8,128)(2,1)S(1)}, bf16[16,1,256,128]{3,2,1,0:T(8,128)(2,1)}, u32[]{:S(2)}) copy-start(bf16[16,1,256,128]{3,2,1,0:T(8,128)(2,1)} %get-tuple-element.112) | copy-start | bytes 3145732
  516.5 17.7 %copy-start.39 = (f32[1,1,4096]{2,0,1:T(1,128)S(1)}, f32[1,1,4096]{2,0,1:T(1,128)}, u32[]{:S(2)}) copy-start(f32[1,1,4096]{2,0,1:T(1,128)} %copy-done.38) | copy-start | bytes 49156
  516.6 17.7 %copy-start.41 = (f32[1,1,4096]{2,0,1:T(1,128)S(1)}, f32[1,1,4096]{2,0,1:T(1,128)}, u32[]{:S(2)}) copy-start(f32[1,1,4096]{2,0,1:T(1,128)} %copy-done.40) | copy-start | bytes 49156
  516.6 17.7 %copy-start.43 = (f32[1,1,4096]{2,0,1:T(1,128)S(1)}, f32[1,1,4096]{2,0,1:T(1,128)}, u32[]{:S(2)}) copy-start(f32[1,1,4096]{2,0,1:T(1,128)} %copy-done.42) | copy-start | bytes 49156
  516.6 17.7 %copy-start.45 = (f32[1,1,4096]{2,0,1:T(1,128)S(1)}, f32[1,1,4096]{2,0,1:T(1,128)}, u32[]{:S(2)}) copy-start(f32[1,1,4096]{2,0,1:T(1,128)} %copy-done.44) | copy-start | bytes 49156
  534.3 11.0 %slice-start.4 = ((s8[6291456]{0:T(1024)(128)(4,1)}), s8[4194304]{0:T(1024)(128)(4,1)S(1)}, s32[]{:S(2)}) async-start(s8[6291456]{0:T(1024)(128)(4,1)} %bitcast.243), calls=%async_computation.12 | async-start | bytes 8388608
  545.4 13.7 %slice-start.10 = ((s8[16777216]{0:T(1024)(128)(4,1)}), s8[4194304]{0:T(1024)(128)(4,1)S(1)}, s32[]{:S(2)}) async-start(s8[16777216]{0:T(1024)(128)(4,1)} %bitcast.319), calls=%async_computation.18 | async-start | bytes 8388608
  550.7 8.4 slice-start.11
  550.7 8.4 slice-start.12
  550.7 9.4 %slice-start.13 = ((s8[16777216]{0:T(1024)(128)(4,1)}), s8[4194304]{0:T(1024)(128)(4,1)S(1)}, s32[]{:S(2)}) async-start(s8[16777216]{0:T(1024)(128)(4,1)} %bitcast.319), calls=%async_computation.21 | async-start | bytes 8388608
  565.4 10.2 %copy-start.28 = (bf16[256,16,128]{2,0,1:T(8,128)(2,1)S(1)}, bf16[256,16,128]{2,0,1:T(8,128)(2,1)}, u32[]{:S(2)}) copy-start(bf16[256,16,128]{2,0,1:T(8,128)(2,1)} %get-tuple-element.101) | copy-start | bytes 3145732
  575.6 284.3 %all-gather.27.cloned.1.call-start = ((), (), s32[]{:S(2)}) async-start(), calls=%async_computation.7 | async-start | bytes 17825792 | tf_op jit(solution)/shard_map/all_gather | solution.py:461
  732.6 13.1 %copy-start.3 = (bf16[3,256,2048]{2,1,0:T(8,128)(2,1)S(1)}, bf16[3,256,2048]{2,1,0:T(8,128)(2,1)}, u32[]{:S(2)}) copy-start(bf16[3,256,2048]{2,1,0:T(8,128)(2,1)} %param.7) | copy-start | bytes 9437188
  732.6 13.1 %copy-start.30 = (bf16[3,256,2048]{1,2,0:T(8,128)(2,1)S(1)}, bf16[3,256,2048]{1,2,0:T(8,128)(2,1)}, u32[]{:S(2)}) copy-start(bf16[3,256,2048]{1,2,0:T(8,128)(2,1)} %pad_maximum_fusion) | copy-start | bytes 9437188
  782.8 14.2 %copy-start.35 = (f32[2048]{0:T(1024)S(1)}, f32[2048]{0:T(1024)}, u32[]{:S(2)}) copy-start(f32[2048]{0:T(1024)} %copy-done.34) | copy-start | bytes 24580
  782.8 14.2 %copy-start.37 = (f32[3,256]{1,0:T(4,128)S(1)}, f32[3,256]{1,0:T(4,128)}, u32[]{:S(2)}) copy-start(f32[3,256]{1,0:T(4,128)} %copy-done.36) | copy-start | bytes 9220
  (38 other events, 137.8 us)
Sparse Core Ops, SparseCore 0:
  15.9 91.0 all-gather.18
  109.2 98.2 all-gather.16
  209.8 124.5 all-gather.20
  474.3 78.0 all-gather.22
  575.7 179.6 all-gather.24
  782.9 76.9 all-gather.26

commit v3 on v2

--- a/solution.py
+++ b/solution.py
@@ -6,6 +6,7 @@
 from jax.experimental.pallas import tpu as pltpu
 from jax.sharding import PartitionSpec as P
 
+
 def flip(me, off, n_dev):
     res, bit = 0, 1
     while bit < n_dev:
@@ -40,7 +41,6 @@
 
 def scatter_kernel(n_dev, part_ref, dst_ref, acc_ref, recv_ref, rs_send, rs_recv, loc_sem, out_sem):
     me = lax.axis_index('sp')
-    rows = part_ref.shape[1]
     orders = reduce_plan(n_dev)
     n_col = len(orders)
     lanes = part_ref.shape[2] // 128
@@ -68,7 +68,7 @@
                                             send_sem=rs_send.at[k], recv_sem=rs_recv.at[k], device_id=(flip(me, bit, n_dev),), device_id_type=pl.DeviceIdType.MESH)
 
     def add(key):
-        c, t, off = key
+        c, _, off = key
         copy(key).wait_recv()
         cols = pl.ds(cuts[c], cuts[c + 1] - cuts[c])
         acc_ref[block(off), :, cols] = acc_ref[block(off), :, cols] + recv_ref[ids[key], :, 0:cuts[c + 1] - cuts[c]]
@@ -173,6 +173,7 @@
             dk_ref[sl, :] = jnp.zeros((blk, head_dim), f32)
             dv_ref[sl, :] = jnp.zeros((blk, head_dim), f32)
             return c
+
         lax.fori_loop(0, n_blk, fill, 0)
 
     q = q_ref[...]
@@ -306,18 +307,20 @@
 
 
 def rows_kernel(piece_ref, out_ref):
-    for j in range(piece_ref.shape[1]):
-        out_ref[:, j * 128:(j + 1) * 128] = piece_ref[0, j]
-
-
-def join_rows(piece):
+    n_grp, lanes, rows, _ = piece_ref.shape
+    for g in range(n_grp):
+        for j in range(lanes):
+            out_ref[g * rows:(g + 1) * rows, j * 128:(j + 1) * 128] = piece_ref[g, j]
+
+
+def join_rows(piece, n_grp=4):
     n_dev, lanes, rows, _ = piece.shape
     return pl.pallas_call(
         rows_kernel,
-        grid=(n_dev,),
+        grid=(n_dev // n_grp,),
         out_shape=jax.ShapeDtypeStruct((n_dev * rows, lanes * 128), piece.dtype),
-        in_specs=[pl.BlockSpec((1, lanes, rows, 128), lambda i: (i, 0, 0, 0))],
-        out_specs=pl.BlockSpec((rows, lanes * 128), lambda i: (i, 0)),
+        in_specs=[pl.BlockSpec((n_grp, lanes, rows, 128), lambda i: (i, 0, 0, 0))],
+        out_specs=pl.BlockSpec((n_grp * rows, lanes * 128), lambda i: (i, 0)),
         compiler_params=pltpu.CompilerParams(dimension_semantics=("arbitrary",)),
         cost_estimate=pl.CostEstimate(flops=piece.size * 16, bytes_accessed=piece.size * 8, transcendentals=0),
         name="join_rows",
@@ -371,6 +374,8 @@
         d_o = jnp.moveaxis(d_o.reshape(n_batch, tok, n_heads, head_dim), 2, 0)
         do_first = lax.all_to_all(d_o[:, 0], 'sp', 0, 0, tiled=True).reshape(seq, head_dim)
 
+        do_rest = d_o[:, 1:].reshape(n_heads, (n_batch - 1) * tok, head_dim)
+
         raw_tok = jnp.einsum('bte,ef->btf', h_act, w_qkv[:, :2 * d_model], preferred_element_type=f32)
         stats_tok = [row_stats(raw_tok[..., n * d_model:(n + 1) * d_model]) for n in range(2)]
         stats_all = lax.all_gather(jnp.stack([s for pair in stats_tok for s in pair]), 'sp')
@@ -391,10 +396,11 @@
             xhat.append(hat)
             q, k = [(hat[n] * ln_head[n]).astype(bf16) for n in range(2)]
             v = raw[:, 2 * head_dim:].astype(bf16)
-            srcs = [d_o[:, a] for a in range(1, n_batch)] if b == 0 else [outs[-1].reshape(n_heads, 4 * tok, head_dim)]
+            srcs = [do_rest] if b == 0 else [outs[-1].reshape(n_heads, 4 * tok, head_dim)]
             out, *got = attention(q, k, v, d_head[b], slope, tok, srcs, b)
             if b == 0:
-                d_head += [t.reshape(seq, head_dim) for t in got]
+                got = got[0].reshape(n_heads, n_batch - 1, tok, head_dim)
+                d_head += [got[:, a].reshape(seq, head_dim) for a in range(n_batch - 1)]
             else:
                 back.append(got[0].reshape(n_heads, 4, tok, head_dim))
             outs.append(out)
@@ -416,14 +422,13 @@
             return jnp.stack(res)
 
         def first_half(lo, hi, nat, mean):
-            y = (jnp.einsum('btd,de->bte', nat[0], w_out, preferred_element_type=f32) + x_f32[lo:hi]).astype(bf16)
             stat = [[s[lo:hi, :, None] for s in pair] for pair in stats_tok]
             hats = [(raw_tok[lo:hi, :, n * d_model:(n + 1) * d_model] - stat[n][0]) * stat[n][1] for n in range(2)]
             grads = [nat[1 + n].astype(f32) for n in range(2)]
             raws = [((grads[n] * ln_flat[n] - mean[2 * n][..., None] - hats[n] * mean[2 * n + 1][..., None]) * stat[n][1]).astype(bf16) for n in range(2)]
             d_qkv = jnp.concatenate(raws + [nat[3]], axis=-1)
             d_h = jnp.einsum('bte,de->btd', d_qkv, w_qkv, preferred_element_type=f32).astype(bf16)
-            return y, d_h, [jnp.sum(grads[n] * hats[n], axis=(0, 1)) for n in range(2)]
+            return d_h, [jnp.sum(grads[n] * hats[n], axis=(0, 1)) for n in range(2)]
 
         def second_half(lo, hi, d_h):
             _, ln1_pull = jax.vjp(layer_norm, x_f32[lo:hi], ln1_f32)
@@ -433,6 +438,8 @@
         last = n_batch - 1
         nat_a = natural(0, last)
         mean_a = token_means(0, last, nat_a)
+        nat_a, mean_a = lax.optimization_barrier((nat_a, mean_a))
+        y_a = (jnp.einsum('btd,de->bte', nat_a[0], w_out, preferred_element_type=f32) + x_f32[:last]).astype(bf16)
         nat_b = natural(last, n_batch)
         mean_b = token_means(last, n_batch, nat_b)
         means_all = lax.all_gather(jnp.concatenate([mean_a, mean_b], axis=1), 'sp')
@@ -456,7 +463,9 @@
         nat = [jnp.concatenate(pair) for pair in zip(nat_a, nat_b)]
         mean = jnp.concatenate([mean_a, mean_b], axis=1)
         w_out_sum, nat, mean = lax.optimization_barrier((w_out_sum, nat, mean))
-        y, d_h, ln_grads = first_half(0, n_batch, nat, mean)
+        y_b = (jnp.einsum('btd,de->bte', nat_b[0], w_out, preferred_element_type=f32) + x_f32[last:]).astype(bf16)
+        y = jnp.concatenate([y_a, y_b])
+        d_h, ln_grads = first_half(0, n_batch, nat, mean)
         w_out_sum, grad_qk, d_h, y = lax.optimization_barrier((w_out_sum, grad_qk, d_h, y))
         w_out_all = lax.all_gather(w_out_sum, 'sp')
         grad_x, grad_ln1 = second_half(0, n_batch, d_h)

time: 895 us -> 912 us (1.019)
    unnamed x156 -> x162, local copies, waits for them, and re-layouts: 17.9 us -> 24.6 us
  transfers between devices with their start and end apart: 8 -> 8, of which waited for: 5 -> 5; matrix products, arithmetic and copies ran while one was open for 33% -> 34% of each run, Pallas kernels for 34% -> 34%
where the time goes in v3:
time: 912 us; the launch traced here: 902 us
  Pallas kernels  386 us (42%)
  matrix products  162 us (18%)
  local copies, waits for them, and re-layouts  95 us (10%)
  waiting for transfers between devices  94.2 us (10%)
  other arithmetic  93.8 us (10%)
  blocking collectives  46 us (5%)
  between operations  15.6 us (2%)
    pallas_call x3, Pallas kernels, attention(): pl.pallas_call(functools.partial(attn_kernel, blk, tok, n_dev, n_src), gr...  211 us
    pallas_call x1, Pallas kernels, reduce_scatter(): pl.pallas_call(functools.partial(scatter_kernel, n_dev), out_shape=jax.Sh...  125 us
    dot_general x6, matrix products, grow(): lax.dot_general(h_all[b], col, (((0,), (0,)), ((), ())), preferred_elemen...  46.9 us
    all_gather x3, waiting for transfers between devices, local_step(): lax.all_gather(h_act[b], 'sp', axis=0, tiled=True)  44.6 us
    all_to_all x1, waiting for transfers between devices, local_step(): back.append(lax.all_to_all(outs[-1], 'sp', 0, 0, tiled=True))  39.5 us
    pallas_call x2, Pallas kernels, place(): pl.pallas_call(functools.partial(place_kernel, n_grp, width), grid=(n_row...  38.3 us
    dot_general x3, matrix products, local_step(): raw = jnp.dot(h_all[b], w_head, preferred_element_type=f32)  36.7 us
    transpose x15, local copies, waits for them, and re-layouts, natural(): jnp.moveaxis(t[:, n], 0, 1).reshape(tok, d_model)  35 us
  transfers between devices with their start and end apart: 8, of which 5 were waited for; matrix products, arithmetic and copies ran while one was open for 34% of the time, Pallas kernels for 34%

profile of v3, /device:TPU:0, one launch (start us, length us, event | category | flops | bytes accessed | tf_op | source)
XLA Modules:
  0.0 901.8 jit_solution(16975156054381000022)
XLA Ops:
  17.7 9.1 %fusion.125 = bf16[3,32,16,8,128]{4,3,2,1,0:T(8,128)(2,1)S(1)} fusion(bf16[3,256,2048]{2,1,0:T(8,128)(2,1)S(1)} %copy-done.26, bf16[2048,2048]{1,0:T(8,128)(2,1)} %param.12), kind=kOutput, calls=%fused_computation.166 | convolution fusion | flops 6444023808 | bytes 14680064 | tf_op jit(solution)/shard_map/bte,fe->btf/dot_general | solution.py:373
  28.7 5.3 all-to-all-start
  35.5 16.9 %fusion.8 = f32[3,256,4096]{2,1,0:T(8,128)S(1)} fusion(bf16[3,256,2048]{2,1,0:T(8,128)(2,1)} %copy-done.11, bf16[2048,6144]{1,0:T(8,128)(2,1)} %param.9), kind=kOutput, calls=%fused_computation.8 | convolution fusion | flops 12884901888 | bytes 32505856 | tf_op jit(solution)/shard_map/bte,ef->btf/dot_general | solution.py:379
  53.1 4.1 copy-done.1
  59.9 14.4 %all-gather.2 = f32[64,3,256]{2,1,0:T(4,128)S(1)} all-gather(f32[4,3,256]{2,1,0:T(4,128)S(1)} %pad_maximum_fusion.8), channel_id=4, replica_groups=mesh['sp'=16] {'sp'}, dimensions={0}, use_global_device_ids=true | all-gather | bytes 208896 | tf_op jit(solution)/shard_map/all_gather | solution.py:381
  78.8 24.3 %all-gather.19.cloned.1.call-done = bf16[1,4096,2048]{2,1,0:T(8,128)(2,1)} async-done(((bf16[1,256,2048]{2,1,0:T(8,128)(2,1)}), bf16[1,4096,2048]{2,1,0:T(8,128)(2,1)}) %all-gather.19.cloned.1.call-update) | async-done | bytes 16777232 | tf_op jit(solution)/shard_map/all_gather | solution.py:371
  103.1 12.6 %fusion.14 = f32[4096,384]{1,0:T(8,128)S(1)} fusion(bf16[1,4096,2048]{2,1,0:T(8,128)(2,1)} %all-gather.19.cloned.1.call-done, bf16[2048,128]{1,0:T(8,128)(2,1)S(1)} %get-tuple-element.84, bf16[2048,128]{1,0:T(8,128)(2,1)S(1)} %get-tuple-element.85, bf16[2048,128]{1,0:T(8,128)(2,1)S(1)} %get-tuple-element.83), kind=kOutput, calls=%fused_computation.14 | convolution fusion | flops 6447169536 | bytes 24641536 | tf_op jit(solution)/shard_map/dot_general | solution.py:394
  118.7 4.2 multiply_convert_fusion.5
  123.0 58.4 %attn_fwd_bwd.3 = (bf16[16,4,256,128]{3,2,1,0:T(8,128)(2,1)}, bf16[16,512,128]{2,1,0:T(8,128)(2,1)}) custom-call(f32[1]{0:T(128)} %dynamic_slice.18.slope_ref, bf16[4096,128]{1,0:T(8,128)(2,1)} %get-tuple-element.99.q_ref, bf16[4096,128]{1,0:T(8,128)(2,1)} %get-tuple-element.98.k_ref, bf16[4096,128]{1,0:T(8,128)(2,1)} %slice.538.v_ref, ...), custom_call_target="tpu_custom_call" | custom-call | flops 28991029248 | bytes 8388608 | tf_op jit(solution)/shard_map/attn_fwd_bwd/pallas_call | solution.py:261
  181.4 18.8 %all-gather.17.cloned.1.call-done = bf16[1,4096,2048]{2,1,0:T(8,128)(2,1)} async-done(((bf16[1,256,2048]{2,1,0:T(8,128)(2,1)}), bf16[1,4096,2048]{2,1,0:T(8,128)(2,1)}) %all-gather.17.cloned.1.call-update) | async-done | bytes 16777232 | tf_op jit(solution)/shard_map/all_gather | solution.py:371
  200.2 12.1 %fusion.20 = f32[4096,384]{1,0:T(8,128)S(1)} fusion(bf16[2048,384]{1,0:T(8,128)(2,1)S(1)} %pad_maximum_fusion.7, bf16[1,4096,2048]{2,1,0:T(8,128)(2,1)} %all-gather.17.cloned.1.call-done), kind=kOutput, calls=%fused_computation.20 | convolution fusion | flops 6442450944 | bytes 24641536 | tf_op jit(solution)/shard_map/dot_general | solution.py:394
  216.9 4.2 multiply_convert_fusion.3
  221.2 88.4 %attn_fwd_bwd.4 = (bf16[16,4,256,128]{3,2,1,0:T(8,128)(2,1)}, bf16[16,1024,128]{2,1,0:T(8,128)(2,1)}) custom-call(f32[1]{0:T(128)} %dynamic_slice.18.slope_ref, bf16[4096,128]{1,0:T(8,128)(2,1)} %get-tuple-element.97.q_ref, bf16[4096,128]{1,0:T(8,128)(2,1)} %get-tuple-element.96.k_ref, bf16[4096,128]{1,0:T(8,128)(2,1)} %slice.537.v_ref, ...), custom_call_target="tpu_custom_call" | custom-call | flops 28991029248 | bytes 8388608 | tf_op jit(solution)/shard_map/attn_fwd_bwd/pallas_call | solution.py:261
  312.8 9.0 fusion.12
  322.0 4.8 fusion.74
  328.2 12.0 %fusion.6 = f32[4096,384]{1,0:T(8,128)S(1)} fusion(bf16[2048,384]{1,0:T(8,128)(2,1)S(1)} %pad_maximum_fusion.7, bf16[1,4096,2048]{2,1,0:T(8,128)(2,1)} %all-gather.21.cloned.1.call-done), kind=kOutput, calls=%fused_computation.6 | convolution fusion | flops 6442450944 | bytes 24641536 | tf_op jit(solution)/shard_map/dot_general | solution.py:394
  341.4 4.9 multiply_convert_fusion.1
  346.4 64.0 %attn_fwd_bwd.5 = (bf16[16,4,256,128]{3,2,1,0:T(8,128)(2,1)}, bf16[16,1024,128]{2,1,0:T(8,128)(2,1)}) custom-call(f32[1]{0:T(128)} %dynamic_slice.18.slope_ref, bf16[4096,128]{1,0:T(8,128)(2,1)} %get-tuple-element.95.q_ref, bf16[4096,128]{1,0:T(8,128)(2,1)} %get-tuple-element.94.k_ref, bf16[4096,128]{1,0:T(8,128)(2,1)} %slice.536.v_ref, ...), custom_call_target="tpu_custom_call" | custom-call | flops 28991029248 | bytes 8388608 | tf_op jit(solution)/shard_map/attn_fwd_bwd/pallas_call | solution.py:261
  413.8 3.5 fusion.139
  417.3 9.3 %fusion.77 = f32[2048,128]{1,0:T(8,128)} fusion(f32[2048,128]{1,0:T(8,128)S(1)} %fusion.74, bf16[4096,128]{1,0:T(8,128)(2,1)S(1)} %bitcast.287, bf16[1,4096,2048]{2,1,0:T(8,128)(2,1)} %all-gather.21.cloned.1.call-done), kind=kOutput, calls=%fused_computation.93 | convolution fusion | flops 2147745792 | bytes 19922944 | tf_op jit(solution)/shard_map/dot_general | solution.py:385
  426.5 39.5 %all-to-all-done.1 = bf16[16,4,256,128]{3,2,1,0:T(8,128)(2,1)} async-done(((bf16[16,4,256,128]{3,2,1,0:T(8,128)(2,1)}), bf16[16,4,256,128]{3,2,1,0:T(8,128)(2,1)}, u32[]{:S(2)}, u32[]{:S(2)}) %all-to-all-start.1) | async-done | bytes 4194336 | tf_op jit(solution)/shard_map/all_to_all | solution.py:407
  466.2 4.0 slice_bitcast_fusion
  471.9 4.3 slice_bitcast_fusion.1
  501.1 6.0 fusion.52
  514.9 3.9 slice_bitcast_fusion.9
  523.8 3.6 fusion.85
  530.0 15.6 %all-gather.4 = f32[64,3,256]{2,1,0:T(4,128)S(1)} all-gather(f32[4,3,256]{2,1,0:T(4,128)S(1)} %maximum_maximum_fusion), channel_id=6, replica_groups=mesh['sp'=16] {'sp'}, dimensions={0}, use_global_device_ids=true | all-gather | bytes 208896 | tf_op jit(solution)/shard_map/all_gather | solution.py:445
  545.9 5.3 fusion.124
  551.3 5.3 fusion.116
  556.6 5.3 fusion.108
  561.9 8.4 fusion.10
  571.3 5.3 fusion.66
  576.7 10.2 %fusion.69 = f32[2048,256]{1,0:T(8,128)} fusion(f32[2048,256]{1,0:T(8,128)S(1)} %fusion.66, bf16[1,4096,2048]{2,1,0:T(8,128)(2,1)} %all-gather.21.cloned.1.call-done, bf16[4096,128]{1,0:T(8,128)(2,1)S(1)} %get-tuple-element.89, bf16[4096,128]{1,0:T(8,128)(2,1)S(1)} %get-tuple-element.88), kind=kOutput, calls=%fused_computation.89 | convolution fusion | flops 4299685888 | bytes 23068672 | tf_op jit(solution)/shard_map/dot_general | solution.py:385
  588.5 12.4 %fusion.46 = bf16[2,256,2048]{2,1,0:T(8,128)(2,1)} fusion(f32[3,256,2048]{2,1,0:T(8,128)S(1)} %convert_element_type.175, bf16[2,256,2048]{1,2,0:T(8,128)(2,1)S(1)} %copy-done.31, bf16[2048,2048]{1,0:T(8,128)(2,1)} %param.12), kind=kOutput, calls=%fused_computation.65 | convolution fusion | flops 4297064448 | bytes 16777216 | tf_op jit(solution)/shard_map/btd,de->bte/dot_general | solution.py:442
  607.8 4.0 pad_maximum_fusion.1
  615.1 3.6 pad_maximum_fusion.3
  618.7 4.1 fusion.73
  626.4 9.6 %convolution_bitcast_fusion = f32[2048,2048]{1,0:T(8,128)} fusion(bf16[3,256,2048]{2,1,0:T(8,128)(2,1)S(1)} %copy-done.27, bf16[1,256,2048]{1,2,0:T(8,128)(2,1)S(1)} %bitcast.269, bf16[2,256,2048]{1,2,0:T(8,128)(2,1)S(1)} %copy-done.32), kind=kOutput, calls=%fused_computation.29 | convolution fusion | flops 6444023808 | bytes 23068672 | tf_op jit(solution)/shard_map/btd,bte->de/dot_general | solution.py:460
  636.1 5.8 copy-done
  641.9 125.0 %sum_scatter.1 = f32[16,128,128]{2,1,0:T(8,128)} custom-call(f32[16,128,2048]{2,1,0:T(8,128)S(1)} %bitcast.254), custom_call_target="tpu_custom_call" | custom-call | flops 10000000 | bytes 33554432 | tf_op jit(solution)/shard_map/sum_scatter/pallas_call | solution.py:120
  766.9 12.2 %fusion.39 = (f32[2048]{0:T(1024)S(1)}, f32[2048]{0:T(1024)S(1)}, bf16[3,256,2048]{2,1,0:T(8,128)(2,1)}, bf16[3,256,2048]{2,1,0:T(8,128)(2,1)}) fusion(bf16[3,256,2048]{2,1,0:T(8,128)(2,1)} %pad_maximum_fusion.1, f32[3,256,4096]{2,1,0:T(8,128)} %copy-done.1, f32[3,256]{1,0:T(4,128)S(1)} %copy-done.61, f32[3,256]{1,0:T(4,128)S(1)} %copy-done.51, ...), kind=kLoop, calls=%fused_computation.47 | loop fusion | flops 34598912 | bytes 25223168 | tf_op jit(solution)/shard_map/reduce_sum | solution.py:431
  779.1 26.6 %fusion.59 = bf16[3,256,2048]{2,1,0:T(8,128)(2,1)} fusion(bf16[2048,6144]{1,0:T(8,128)(2,1)} %param.9, bf16[3,256,2048]{2,1,0:T(8,128)(2,1)} %pad_maximum_fusion.3, bf16[3,256,2048]{2,1,0:T(8,128)(2,1)} %get-tuple-element.86, bf16[3,256,2048]{2,1,0:T(8,128)(2,1)} %get-tuple-element.87), kind=kOutput, calls=%fused_computation.80 | convolution fusion | flops 19357237248 | bytes 37748736 | tf_op jit(solution)/shard_map/bte,de->btd/dot_general | solution.py:430
  805.7 14.4 %place_cols.2.refs_0_ = f32[2048,6144]{1,0:T(8,128)} custom-call(f32[16,2048,128]{2,1,0:T(8,128)} %bitcast.259), custom_call_target="tpu_custom_call" | custom-call | flops 67108864 | bytes 33554432 | tf_op jit(solution)/shard_map/place_cols/pallas_call | solution.py:296
  826.9 16.0 %all-gather.9 = f32[16,3,2048]{2,1,0:T(4,128)} all-gather(f32[1,3,2048]{2,1,0:T(4,128)S(1)} %maximum_bitcast_fusion), channel_id=9, replica_groups=mesh['sp'=16] {'sp'}, dimensions={0}, use_global_device_ids=true | all-gather | bytes 417792 | tf_op jit(solution)/shard_map/all_gather | solution.py:472
  844.0 23.9 %place_cols.3 = f32[2048,6144]{1,0:T(8,128)} custom-call(f32[16,2048,256]{2,1,0:T(8,128)} %bitcast.255, f32[2048,6144]{1,0:T(8,128)} %place_cols.2.refs_0_), custom_call_target="tpu_custom_call", output_to_operand_aliasing={{}: (1, {})} | custom-call | flops 134217728 | bytes 67108864 | tf_op jit(solution)/shard_map/place_cols/pallas_call | solution.py:296
  868.6 5.8 add_convert_fusion
  874.4 8.7 all-gather.27.cloned.1.call-done
  883.1 11.7 %join_rows.1 = f32[2048,2048]{1,0:T(8,128)} custom-call(f32[16,16,128,128]{3,2,1,0:T(8,128)} %bitcast.258), custom_call_target="tpu_custom_call" | custom-call | flops 67108864 | bytes 33554432 | tf_op jit(solution)/shard_map/join_rows/pallas_call | solution.py:318
  (272 shorter events, 105.4 us)
Async XLA Ops:
  7.2 95.9 %all-gather.19.cloned.1.call-start = ((), (), s32[]{:S(2)}) async-start(), calls=%async_computation.3 | async-start | bytes 17825792 | tf_op jit(solution)/shard_map/all_gather | solution.py:371
  15.8 184.4 %all-gather.17.cloned.1.call-start = ((), (), s32[]{:S(2)}) async-start(), calls=%async_computation.2 | async-start | bytes 17825792 | tf_op jit(solution)/shard_map/all_gather | solution.py:371
  16.6 311.7 %all-gather.21.cloned.1.call-start = ((), (), s32[]{:S(2)}) async-start(), calls=%async_computation.4 | async-start | bytes 17825792 | tf_op jit(solution)/shard_map/all_gather | solution.py:371
  28.7 94.2 %all-to-all-start = ((bf16[16,256,128]{2,1,0:T(8,128)(2,1)}), bf16[16,256,128]{2,1,0:T(8,128)(2,1)}, u32[]{:S(2)}, u32[]{:S(2)}) async-start(bf16[16,256,128]{2,1,0:T(8,128)(2,1)} %slice_bitcast_fusion.8), calls=%async_computation | async-start | bytes 2097152 | tf_op jit(solution)/shard_map/all_to_all | solution.py:375
  57.2 17.9 %copy-start.62 = (bf16[16,128]{1,0:T(8,128)(2,1)S(1)}, bf16[16,128]{1,0:T(8,128)(2,1)}, u32[]{:S(2)}) copy-start(bf16[16,128]{1,0:T(8,128)(2,1)} %param.10) | copy-start | bytes 12292
  57.2 18.5 %copy-start.63 = (bf16[16,128]{1,0:T(8,128)(2,1)S(1)}, bf16[16,128]{1,0:T(8,128)(2,1)}, u32[]{:S(2)}) copy-start(bf16[16,128]{1,0:T(8,128)(2,1)} %param.11) | copy-start | bytes 12292
  78.7 38.2 %copy-start.38 = (f32[1,1,4096]{2,0,1:T(1,128)}, f32[1,1,4096]{2,0,1:T(1,128)S(1)}, u32[]{:S(2)}) copy-start(f32[1,1,4096]{2,0,1:T(1,128)S(1)} %get-tuple-element.145) | copy-start | bytes 49156
  78.8 38.2 %copy-start.40 = (f32[1,1,4096]{2,0,1:T(1,128)}, f32[1,1,4096]{2,0,1:T(1,128)S(1)}, u32[]{:S(2)}) copy-start(f32[1,1,4096]{2,0,1:T(1,128)S(1)} %get-tuple-element.146) | copy-start | bytes 49156
  78.8 38.2 %copy-start.42 = (f32[1,1,4096]{2,0,1:T(1,128)}, f32[1,1,4096]{2,0,1:T(1,128)S(1)}, u32[]{:S(2)}) copy-start(f32[1,1,4096]{2,0,1:T(1,128)S(1)} %get-tuple-element.147) | copy-start | bytes 49156
  78.8 38.2 %copy-start.44 = (f32[1,1,4096]{2,0,1:T(1,128)}, f32[1,1,4096]{2,0,1:T(1,128)S(1)}, u32[]{:S(2)}) copy-start(f32[1,1,4096]{2,0,1:T(1,128)S(1)} %get-tuple-element.148) | copy-start | bytes 49156
  221.2 89.9 %copy-start.28 = (bf16[16,4,256,128]{3,2,1,0:T(8,128)(2,1)S(1)}, bf16[16,4,256,128]{3,2,1,0:T(8,128)(2,1)}, u32[]{:S(2)}) copy-start(bf16[16,4,256,128]{3,2,1,0:T(8,128)(2,1)} %get-tuple-element.40) | copy-start | bytes 12582916
  309.6 12.2 %slice-start.8 = ((s8[16777216]{0:T(1024)(128)(4,1)}), s8[4194304]{0:T(1024)(128)(4,1)S(1)}, s32[]{:S(2)}) async-start(s8[16777216]{0:T(1024)(128)(4,1)} %bitcast.340), calls=%async_computation.16 | async-start | bytes 8388608
  311.1 10.7 %slice-start.9 = ((s8[16777216]{0:T(1024)(128)(4,1)}), s8[4194304]{0:T(1024)(128)(4,1)S(1)}, s32[]{:S(2)}) async-start(s8[16777216]{0:T(1024)(128)(4,1)} %bitcast.340), calls=%async_computation.17 | async-start | bytes 8388608
  312.8 9.0 slice-start.10
  312.8 9.2 %slice-start.11 = ((s8[16777216]{0:T(1024)(128)(4,1)}), s8[4194304]{0:T(1024)(128)(4,1)S(1)}, s32[]{:S(2)}) async-start(s8[16777216]{0:T(1024)(128)(4,1)} %bitcast.340), calls=%async_computation.19 | async-start | bytes 8388608
  340.3 6.1 copy-start.7
  410.4 55.6 %all-to-all-start.1 = ((bf16[16,4,256,128]{3,2,1,0:T(8,128)(2,1)}), bf16[16,4,256,128]{3,2,1,0:T(8,128)(2,1)}, u32[]{:S(2)}, u32[]{:S(2)}) async-start(bf16[16,4,256,128]{3,2,1,0:T(8,128)(2,1)} %get-tuple-element.47), calls=%async_computation.1 | async-start | bytes 8388608 | tf_op jit(solution)/shard_map/all_to_all | solution.py:407
  413.7 173.1 %all-gather.23.cloned.1.call-start = ((), (), s32[]{:S(2)}) async-start(), calls=%async_computation.5 | async-start | bytes 17825792 | tf_op jit(solution)/shard_map/all_gather | solution.py:411
  417.3 48.8 %copy-start.51 = (f32[3,256]{1,0:T(4,128)S(1)}, f32[3,256]{1,0:T(4,128)}, u32[]{:S(2)}) copy-start(f32[3,256]{1,0:T(4,128)} %copy-done.50) | copy-start | bytes 9220
  417.3 48.8 %copy-start.53 = (f32[3,256]{1,0:T(4,128)S(1)}, f32[3,256]{1,0:T(4,128)}, u32[]{:S(2)}) copy-start(f32[3,256]{1,0:T(4,128)} %copy-done.52) | copy-start | bytes 9220
  417.3 48.8 %copy-start.61 = (f32[3,256]{1,0:T(4,128)S(1)}, f32[3,256]{1,0:T(4,128)}, u32[]{:S(2)}) copy-start(f32[3,256]{1,0:T(4,128)} %get-tuple-element.162) | copy-start | bytes 9220
  417.3 48.9 %copy-start.60 = (f32[3,256]{1,0:T(4,128)S(1)}, f32[3,256]{1,0:T(4,128)}, u32[]{:S(2)}) copy-start(f32[3,256]{1,0:T(4,128)} %get-tuple-element.158) | copy-start | bytes 9220
  466.0 339.7 %all-gather.25.cloned.1.call-start = ((), (), s32[]{:S(2)}) async-start(), calls=%async_computation.6 | async-start | bytes 35651584 | tf_op jit(solution)/shard_map/all_gather | solution.py:457
  500.9 6.2 copy-start.10
  501.0 6.1 copy-start.22
  501.0 6.1 copy-start.23
  519.9 7.5 copy-start.13
  521.3 24.5 %slice-start.2 = ((s8[6291456]{0:T(1024)(128)(4,1)}), s8[2097152]{0:T(1024)(128)(4,1)S(1)}, s32[]{:S(2)}) async-start(s8[6291456]{0:T(1024)(128)(4,1)} %bitcast.260), calls=%async_computation.10 | async-start | bytes 4194304
  523.8 22.1 %slice-start.3 = ((s8[6291456]{0:T(1024)(128)(4,1)}), s8[4194304]{0:T(1024)(128)(4,1)S(1)}, s32[]{:S(2)}) async-start(s8[6291456]{0:T(1024)(128)(4,1)} %bitcast.260), calls=%async_computation.11 | async-start | bytes 8388608
  523.8 27.4 %slice-start.4 = ((s8[6291456]{0:T(1024)(128)(4,1)}), s8[2097152]{0:T(1024)(128)(4,1)S(1)}, s32[]{:S(2)}) async-start(s8[6291456]{0:T(1024)(128)(4,1)} %bitcast.262), calls=%async_computation.12 | async-start | bytes 4194304
  527.4 18.4 %copy-start.16 = (bf16[16,1,256,128]{3,2,1,0:T(8,128)(2,1)S(1)}, bf16[16,1,256,128]{3,2,1,0:T(8,128)(2,1)}, u32[]{:S(2)}) copy-start(bf16[16,1,256,128]{3,2,1,0:T(8,128)(2,1)} %get-tuple-element.109) | copy-start | bytes 3145732
  527.4 18.4 %copy-start.17 = (bf16[16,1,256,128]{3,2,1,0:T(8,128)(2,1)S(1)}, bf16[16,1,256,128]{3,2,1,0:T(8,128)(2,1)}, u32[]{:S(2)}) copy-start(bf16[16,1,256,128]{3,2,1,0:T(8,128)(2,1)} %get-tuple-element.110) | copy-start | bytes 3145732
  527.5 18.4 %copy-start.39 = (f32[1,1,4096]{2,0,1:T(1,128)S(1)}, f32[1,1,4096]{2,0,1:T(1,128)}, u32[]{:S(2)}) copy-start(f32[1,1,4096]{2,0,1:T(1,128)} %copy-done.38) | copy-start | bytes 49156
  527.5 18.4 %copy-start.41 = (f32[1,1,4096]{2,0,1:T(1,128)S(1)}, f32[1,1,4096]{2,0,1:T(1,128)}, u32[]{:S(2)}) copy-start(f32[1,1,4096]{2,0,1:T(1,128)} %copy-done.40) | copy-start | bytes 49156
  527.5 18.4 %copy-start.43 = (f32[1,1,4096]{2,0,1:T(1,128)S(1)}, f32[1,1,4096]{2,0,1:T(1,128)}, u32[]{:S(2)}) copy-start(f32[1,1,4096]{2,0,1:T(1,128)} %copy-done.42) | copy-start | bytes 49156
  527.5 18.4 %copy-start.45 = (f32[1,1,4096]{2,0,1:T(1,128)S(1)}, f32[1,1,4096]{2,0,1:T(1,128)}, u32[]{:S(2)}) copy-start(f32[1,1,4096]{2,0,1:T(1,128)} %copy-done.44) | copy-start | bytes 49156
  545.9 10.6 %slice-start.6 = ((s8[6291456]{0:T(1024)(128)(4,1)}), s8[4194304]{0:T(1024)(128)(4,1)S(1)}, s32[]{:S(2)}) async-start(s8[6291456]{0:T(1024)(128)(4,1)} %bitcast.264), calls=%async_computation.14 | async-start | bytes 8388608
  556.6 13.7 %slice-start.12 = ((s8[16777216]{0:T(1024)(128)(4,1)}), s8[4194304]{0:T(1024)(128)(4,1)S(1)}, s32[]{:S(2)}) async-start(s8[16777216]{0:T(1024)(128)(4,1)} %bitcast.342), calls=%async_computation.20 | async-start | bytes 8388608
  561.9 8.4 slice-start.13
  561.9 8.4 slice-start.14
  561.9 9.4 %slice-start.15 = ((s8[16777216]{0:T(1024)(128)(4,1)}), s8[4194304]{0:T(1024)(128)(4,1)S(1)}, s32[]{:S(2)}) async-start(s8[16777216]{0:T(1024)(128)(4,1)} %bitcast.342), calls=%async_computation.23 | async-start | bytes 8388608
  576.6 10.3 %copy-start.3 = (bf16[3,256,2048]{2,1,0:T(8,128)(2,1)S(1)}, bf16[3,256,2048]{2,1,0:T(8,128)(2,1)}, u32[]{:S(2)}) copy-start(bf16[3,256,2048]{2,1,0:T(8,128)(2,1)} %param.7) | copy-start | bytes 9437188
  586.9 296.2 %all-gather.27.cloned.1.call-start = ((), (), s32[]{:S(2)}) async-start(), calls=%async_computation.7 | async-start | bytes 17825792 | tf_op jit(solution)/shard_map/all_gather | solution.py:470
  588.5 12.4 %copy-start.12 = (f32[3,256,2048]{2,1,0:T(8,128)}, f32[3,256,2048]{2,1,0:T(8,128)S(1)}, u32[]{:S(2)}) copy-start(f32[3,256,2048]{2,1,0:T(8,128)S(1)} %convert_element_type.175) | copy-start | bytes 18874372
  607.8 10.9 %slice-start = ((s8[8388608]{0:T(1024)(128)(4,1)}), s8[4194304]{0:T(1024)(128)(4,1)S(1)}, s32[]{:S(2)}) async-start(s8[8388608]{0:T(1024)(128)(4,1)} %bitcast.256), calls=%async_computation.8 | async-start | bytes 8388608
  611.8 6.8 slice-start.1
  805.7 14.4 %copy-start.35 = (f32[2048]{0:T(1024)S(1)}, f32[2048]{0:T(1024)}, u32[]{:S(2)}) copy-start(f32[2048]{0:T(1024)} %copy-done.34) | copy-start | bytes 24580
  805.7 14.4 %copy-start.37 = (f32[3,256]{1,0:T(4,128)S(1)}, f32[3,256]{1,0:T(4,128)}, u32[]{:S(2)}) copy-start(f32[3,256]{1,0:T(4,128)} %copy-done.36) | copy-start | bytes 9220
  (40 other events, 140.8 us)
Sparse Core Ops, SparseCore 0:
  15.9 87.1 all-gather.18
  105.3 94.8 all-gather.16
  202.5 125.7 all-gather.20
  466.1 78.5 all-gather.22
  587.0 186.4 all-gather.24
  805.8 77.2 all-gather.26
